TPU v7x, 128 devices: a whole 4x4x4 slice. The times are simulated.
128 devices in a mesh: ka: 16 (over z_lo, y, core), ga: 8 (over x, z_hi).
Axes of the slice: x: 4, y: 4, z: 4 (z_hi: 2, z_lo: 2; z = z_hi * 2 + z_lo), core: 2. Of those that a mesh axis runs over, the one named last changes fastest.
Arguments:
- coeffs: bfloat16 [16, 2, 15360, 256], P('ka', None, 'ga'), may hold values from -1 to 1
- projectors: bfloat16 [2, 15360, 1024], P(None, 'ga'), may hold values from -1.5 to 1.5
- proj_deriv: bfloat16 [2, 15360, 1024], P(None, 'ga'), may hold values from -1.5 to 1.5
- shift_map: int32 [15360], P('ga'), may hold values from 0 to 15359, as said below
- atom_of: int32 [1024], replicated, may hold values from 0 to 127, as said below
Outputs:
- transport: float32 [16, 2, 256, 256], P('ka')
- forces: float32 [128], replicated
Inputs may be any that keep to these rules, and one draw needn't show every extreme that they name: `shift_map`: a permutation that maps each aligned block of 1920 plane waves onto itself. `atom_of`: each atom owns exactly 8 projectors.
All inputs are finite; a program needn't handle non-finite values.
Results may differ from a plain program's by a relative error of at most 0.0003.
Values may be sent and summed in bfloat16 or wider, within the bound.
A program may use at most 128 MiB of HBM per device.

v0:
```python
import functools

import jax
import jax.numpy as jnp
from jax import lax
from jax.sharding import Mesh
from jax.sharding import PartitionSpec as P

NA = 128
NEWTON = 2
KA = ("ka_0", "ka_1", "ka_2")
GA = ("ga_0", "ga_1")
KA_GA = ("ka_0", "ka_1", "ka_2", "ga_0", "ga_1")


def from_behind(block, axis, distance):
    devices = range(lax.axis_size(axis))
    route = [((i - distance) % len(devices), i) for i in devices]
    return lax.ppermute(block, axis, route)


def total_of_pieces(shard, axis):
    pieces = lax.all_gather(shard, axis)
    return pieces.sum(axis=0)


def in_one_piece(arrays, axis, dim, along):
    widths = [a.shape[along] for a in arrays]
    both = jnp.concatenate(arrays, axis=along)
    filled = lax.psum_scatter(both, axis, scatter_dimension=dim, tiled=True)
    return tuple(jnp.split(filled, [sum(widths[:k]) for k in range(1, len(widths))], axis=along))


def prefix(value, axis, join, neutral):
    count, mine = (lax.axis_size(axis), lax.axis_index(axis))
    pieces = lax.all_gather(value, axis)
    subtotal = jnp.full_like(value, 0) + jnp.asarray(neutral, value.dtype)

    def step(position, subtotal):
        longer = join(subtotal, pieces[position])
        return jnp.where(position < mine, longer, subtotal)

    return lax.fori_loop(0, count - 1, step, subtotal)


def by_axis(shard, axes):
    return functools.reduce(lax.psum, axes, shard)


def cmul(left, right):
    highest = lax.Precision.HIGHEST
    left_re, left_im = (left[..., 0, :, :], left[..., 1, :, :])
    right_re, right_im = (right[..., 0, :, :], right[..., 1, :, :])
    real_part = jnp.matmul(left_re, right_re, precision=highest) - jnp.matmul(
        left_im, right_im, precision=highest
    )
    imag_part = jnp.matmul(left_re, right_im, precision=highest) + jnp.matmul(
        left_im, right_re, precision=highest
    )
    return jnp.stack([real_part, imag_part], axis=-3)


def invert(intersection, eye_c):
    estimate = jnp.broadcast_to(eye_c, intersection.shape)
    for newton_step in range(NEWTON):
        estimate = cmul(estimate, 2.0 * eye_c - cmul(intersection, estimate))
    return estimate


def project(proj_table, columns, swapped):
    real_part = jnp.einsum("gp,kgn->kpn", proj_table, columns, preferred_element_type=jnp.float32)
    imag_part = jnp.einsum("gp,kgn->kpn", proj_table, swapped, preferred_element_type=jnp.float32)
    return jnp.stack([real_part, imag_part], axis=1)


def local(coeffs, projectors, proj_deriv, shift_map, atom_of):
    points_here = coeffs.shape[0]
    plane_rows = coeffs.shape[2]
    bands = coeffs.shape[3]
    string_devices = lax.axis_size(KA)
    position = lax.axis_index(KA)
    total_points = points_here * string_devices
    eye_c = jnp.stack([jnp.eye(bands, dtype=jnp.float32), jnp.zeros((bands, bands), jnp.float32)])
    arrived = from_behind(coeffs[0], KA, -1)
    local_map = shift_map % plane_rows
    wrapped = jnp.where(position == string_devices - 1, arrived[:, local_map, :], arrived)
    following = jnp.concatenate([coeffs[1:], wrapped[None]], axis=0)
    columns = coeffs.reshape(points_here, 2 * plane_rows, bands)
    own_swap = jnp.concatenate([coeffs[:, 1], -coeffs[:, 0]], axis=1)
    next_cols = following.reshape(points_here, 2 * plane_rows, bands)
    next_swap = jnp.concatenate([following[:, 1], -following[:, 0]], axis=1)
    batch_dims = (((1,), (1,)), ((0,), (0,)))
    intersection_part = jnp.stack(
        [
            lax.dot_general(columns, next_cols, batch_dims, preferred_element_type=jnp.float32),
            lax.dot_general(columns, next_swap, batch_dims, preferred_element_type=jnp.float32),
        ],
        axis=1,
    )
    proj_table = projectors.reshape(2 * plane_rows, projectors.shape[2])
    deriv_table = proj_deriv.reshape(2 * plane_rows, proj_deriv.shape[2])
    proj_part = project(proj_table, columns, own_swap)
    deriv_part = project(deriv_table, columns, own_swap)
    intersections = total_of_pieces(intersection_part, GA)
    proj_vals, deriv_vals = in_one_piece((proj_part, deriv_part), GA, 2, 0)
    share_rows = proj_vals.shape[2]
    atom_ids = lax.dynamic_slice_in_dim(atom_of, lax.axis_index(GA) * share_rows, share_rows, 0)
    inverses = invert(intersections, eye_c)
    chain_list = [inverses[0]]
    local_chain = jnp.stack(chain_list)
    device_product = chain_list[-1]
    offset = prefix(device_product, KA, cmul, eye_c)
    transport = cmul(offset[None], local_chain)
    weighted = cmul(proj_vals, transport)
    per_proj = (
        jnp.sum(deriv_vals[:, 0] * weighted[:, 1] - deriv_vals[:, 1] * weighted[:, 0], axis=(0, 2))
        / total_points
    )
    onehot = (atom_ids[None, :] == jnp.arange(NA, dtype=jnp.int32)[:, None]).astype(jnp.float32)
    force_part = jnp.dot(onehot, per_proj, precision=lax.Precision.HIGHEST)
    forces = by_axis(force_part, KA_GA)
    return (transport, forces)


def solution(mesh):
    torus = Mesh(mesh.devices.reshape(2, 4, 2, 4, 2), ("ka_0", "ka_1", "ka_2", "ga_0", "ga_1"))
    in_specs = (P(KA, None, GA, None), P(None, GA, None), P(None, GA, None), P(GA), P())
    out_specs = (P(KA, None, None, None), P())
    return jax.shard_map(local, mesh=torus, in_specs=in_specs, out_specs=out_specs, check_vma=False)
```

profile of v0, /device:TPU:0, one launch (start us, length us, event | category | flops | bytes accessed | tf_op | source)
XLA Modules:
  0.0 350.2 jit_solution(16242457775778894116)
XLA Ops:
  7.2 15.5 %copy.44 = bf16[1,2,1920,256]{3,1,2,0:T(2,128)(2,1)} copy(bf16[1,2,1920,256]{3,2,1,0:T(8,128)(2,1)} %param.7) | data formatting | bytes 3932160 | tf_op args[0]
  22.7 3.9 %collective-permute-start = (bf16[2,1920,256]{2,0,1:T(2,128)(2,1)}, bf16[2,1920,256]{2,0,1:T(2,128)(2,1)S(1)}, u32[]{:S(2)}, u32[]{:S(2)}) collective-permute-start(bf16[2,1920,256]{2,0,1:T(2,128)(2,1)} %bitcast.198), channel_id=1, source_target_pairs={{8,0},{16,8},{24,16},{32,24},{40,32},{48,40},{56,48},{64,56},{72,6... | collective-permute-start | bytes 5898248 | tf_op jit(solution)/shard_map/ppermute | solution.py:19
  26.7 22.4 %collective-permute-done = bf16[2,1920,256]{2,0,1:T(2,128)(2,1)S(1)} collective-permute-done((bf16[2,1920,256]{2,0,1:T(2,128)(2,1)}, bf16[2,1920,256]{2,0,1:T(2,128)(2,1)S(1)}, u32[]{:S(2)}, u32[]{:S(2)}) %collective-permute-start) | collective-permute-done | bytes 1966112 | tf_op jit(solution)/shard_map/ppermute | solution.py:19
  49.1 8.3 %gather_fusion = bf16[1920,2,256]{2,1,0:T(2,128)(2,1)} fusion(bf16[2,1920,256]{2,0,1:T(2,128)(2,1)S(1)} %collective-permute-done, s32[2048]{0:T(1024)S(1)} %pad_clamp_fusion), kind=kCustom, calls=%fused_computation | custom fusion | bytes 3939840 | tf_op jit(solution)/shard_map/gather | solution.py:86
  57.4 3.7 %broadcast_select_fusion = bf16[2,1920,256]{2,0,1:T(2,128)(2,1)S(1)} fusion(bf16[2,1920,256]{2,0,1:T(2,128)(2,1)S(1)} %collective-permute-done, pred[]{:T(512)S(6)} %eq.29, bf16[1920,2,256]{2,1,0:T(2,128)(2,1)} %gather_fusion), kind=kLoop, calls=%fused_computation.23 | loop fusion | flops 983040 | bytes 5898241 | tf_op jit(solution)/shard_map/jit(_where)/select_n | solution.py:86
  61.3 3.6 %fusion.50 = (bf16[1,1,1920,256]{3,1,2,0:T(2,128)(2,1)S(1)}, bf16[1,1,1920,256]{3,1,2,0:T(2,128)(2,1)S(1)}) fusion(bf16[1,2,1920,256]{3,1,2,0:T(2,128)(2,1)S(1)} %bitcast.227), kind=kLoop, calls=%fused_computation.110 | loop fusion | flops 491520 | bytes 3932160 | tf_op jit(solution)/shard_map/slice | solution.py:91
  70.2 72.4 %all-gather.6.cloned.1.call-done = f32[8,2,256,256]{3,2,1,0:T(8,128)} async-done(((f32[1,2,256,256]{3,2,1,0:T(8,128)}), f32[8,2,256,256]{3,2,1,0:T(8,128)}) %all-gather.6.cloned.1.call-update) | async-done | bytes 4194320 | tf_op jit(solution)/shard_map/all_gather | solution.py:23
  142.6 2.5 reduce.3
  153.5 5.6 %convolution_bitcast_fusion = f32[1,1,1024,256]{2,3,1,0:T(8,128)S(1)} fusion(bf16[3840,1024]{1,0:T(8,128)(2,1)} %bitcast.228, bf16[1,1920,256]{2,1,0:T(8,128)(2,1)S(1)} %get-tuple-element.111, bf16[1,1920,256]{2,1,0:T(8,128)(2,1)S(1)} %get-tuple-element.110), kind=kOutput, calls=%fused_computation.31 | convolution fusion | flops 2017198080 | bytes 10878976 | tf_op jit(solution)/shard_map/gp,kgn->kpn/dot_general | solution.py:72
  159.2 2.2 convolution_bitcast_fusion.2
  161.8 2.2 convolution_bitcast_fusion.1
  164.0 2.2 convolution_bitcast_fusion.3
  166.3 2.5 maximum_maximum_fusion
  170.8 32.3 %all-gather.4.cloned.1.call-done = f32[16,2,256,256]{3,2,1,0:T(8,128)} async-done(((f32[1,2,256,256]{3,2,1,0:T(8,128)}), f32[16,2,256,256]{3,2,1,0:T(8,128)}) %all-gather.4.cloned.1.call-update) | async-done | bytes 8388624 | tf_op jit(solution)/shard_map/all_gather | solution.py:36
  203.0 96.0 %while.13 = (s32[]{:T(128)}, f32[2,256,256]{1,2,0:T(8,128)S(1)}, s32[]{:T(128)}, f32[16,2,256,256]{3,2,1,0:T(8,128)}, s32[]{:T(128)}, /*index=5*/s32[]{:T(128)}, s32[]{}) while((s32[]{:T(128)}, f32[2,256,256]{1,2,0:T(8,128)S(1)}, s32[]{:T(128)}, f32[16,2,256,256]{3,2,1,0:T(8,128)}, s32[]{:T(128)}, /*index=5*/s32[]{:T(128)}, s32[]{}) %tuple.41), condition=%wide.region_2.3_spmd, body=%wide.region_1.2_spmd.sunk | while | flops 805699584 | bytes 5245035 | solution.py:43
  207.7 1.6 fusion.91
  211.0 1.6 fusion.89
  217.4 1.6 fusion.89
  223.8 1.6 fusion.89
  226.9 1.6 fusion.91
  228.6 1.6 fusion.88
  230.2 1.6 fusion.89
  233.3 1.6 fusion.91
  235.0 1.6 fusion.88
  236.6 1.6 fusion.89
  239.7 1.6 fusion.91
  241.4 1.6 fusion.88
  243.0 1.6 fusion.89
  244.5 1.6 fusion.90
  246.1 1.6 fusion.91
  252.5 1.6 fusion.91
  255.8 1.6 fusion.89
  258.9 1.6 fusion.91
  263.7 1.6 fusion.90
  265.3 1.6 fusion.91
  275.0 1.6 fusion.89
  278.1 1.6 fusion.91
  284.5 1.6 fusion.91
  287.8 1.6 fusion.89
  289.3 1.6 fusion.90
  290.9 1.6 fusion.91
  304.4 1.6 fusion.26
  306.0 1.6 fusion.27
  307.7 5.0 %psum.35 = f32[128]{0:T(128)S(1)} all-reduce(f32[128]{0:T(128)S(1)} %convolution_bitcast_fusion.5), channel_id=1, replica_groups=mesh['ka_0'=2,'ka_1'=4,'ka_2'=2,'ga_0'=4,'ga_1'=2] {'ka_0'}, use_global_device_ids=true, to_apply=%region_5.6 | all-reduce | flops 128 | bytes 1024 | tf_op jit(solution)/shard_map/psum | solution.py:47
  312.7 10.4 %psum.36 = f32[128]{0:T(128)S(1)} all-reduce(f32[128]{0:T(128)S(1)} %psum.35), channel_id=1, replica_groups=mesh['ka_0'=2,'ka_1'=4,'ka_2'=2,'ga_0'=4,'ga_1'=2] {'ka_1'}, use_global_device_ids=true, to_apply=%region_6.7 | all-reduce | flops 128 | bytes 1024 | tf_op jit(solution)/shard_map/psum | solution.py:47
  323.1 2.5 psum.37
  325.5 10.4 %psum.38 = f32[128]{0:T(128)S(1)} all-reduce(f32[128]{0:T(128)S(1)} %psum.37), channel_id=1, replica_groups=mesh['ka_0'=2,'ka_1'=4,'ka_2'=2,'ga_0'=4,'ga_1'=2] {'ga_0'}, use_global_device_ids=true, to_apply=%region_8.9 | all-reduce | flops 128 | bytes 1024 | tf_op jit(solution)/shard_map/psum | solution.py:47
  335.9 6.9 %psum.39 = f32[128]{0:T(128)} all-reduce(f32[128]{0:T(128)S(1)} %psum.38), channel_id=1, replica_groups=mesh['ka_0'=2,'ka_1'=4,'ka_2'=2,'ga_0'=4,'ga_1'=2] {'ga_1'}, use_global_device_ids=true, to_apply=%region_9.10 | all-reduce | flops 128 | bytes 1024 | tf_op jit(solution)/shard_map/psum | solution.py:47
  (113 shorter events, 77.1 us)
Async XLA Ops:
  7.2 19.5 %copy-start.2 = (s32[1920]{0:T(1024)S(1)}, s32[1920]{0:T(1024)}, u32[]{:S(2)}) copy-start(s32[1920]{0:T(1024)} %param.10) | copy-start | bytes 23044
  7.2 135.4 %all-gather.6.cloned.1.call-start = ((), (), s32[]{:S(2)}) async-start(), calls=%async_computation.3 | async-start | bytes 4718592 | tf_op jit(solution)/shard_map/all_gather | solution.py:23
  22.7 26.4 %collective-permute-start = (bf16[2,1920,256]{2,0,1:T(2,128)(2,1)}, bf16[2,1920,256]{2,0,1:T(2,128)(2,1)S(1)}, u32[]{:S(2)}, u32[]{:S(2)}) collective-permute-start(bf16[2,1920,256]{2,0,1:T(2,128)(2,1)} %bitcast.198), channel_id=1, source_target_pairs={{8,0},{16,8},{24,16},{32,24},{40,32},{48,40},{56,48},{64,56},{72,6... | collective-permute-start | bytes 5898248 | tf_op jit(solution)/shard_map/ppermute | solution.py:19
  65.0 1.5 copy-start
  69.0 134.0 %all-gather.4.cloned.1.call-start = ((), (), s32[]{:S(2)}) async-start(), calls=%async_computation.1 | async-start | bytes 8912896 | tf_op jit(solution)/shard_map/all_gather | solution.py:36
  153.1 148.3 %reduce-scatter.2.cloned.1.call-start = ((), (), s32[]{:S(2)}) async-start(), calls=%async_computation.2 | async-start | bytes 4718592 | tf_op jit(solution)/shard_map/reduce_scatter | solution.py:30
  153.4 5.8 %slice-start.2 = ((s8[7864320]{0:T(1024)(128)(4,1)}), s8[4194304]{0:T(1024)(128)(4,1)S(1)}, s32[]{:S(2)}) async-start(s8[7864320]{0:T(1024)(128)(4,1)} %bitcast.232), calls=%async_computation.6 | async-start | bytes 8388608
  153.5 5.7 %slice-start.3 = ((s8[7864320]{0:T(1024)(128)(4,1)}), s8[3670016]{0:T(1024)(128)(4,1)S(1)}, s32[]{:S(2)}) async-start(s8[7864320]{0:T(1024)(128)(4,1)} %bitcast.232), calls=%async_computation.7 | async-start | bytes 7340032
  153.5 7.9 %slice-start = ((s8[7864320]{0:T(1024)(128)(4,1)}), s8[4194304]{0:T(1024)(128)(4,1)S(1)}, s32[]{:S(2)}) async-start(s8[7864320]{0:T(1024)(128)(4,1)} %bitcast.229), calls=%async_computation.4 | async-start | bytes 8388608
  159.2 2.6 slice-start.1
  168.7 1.1 copy-start.1
Sparse Core Ops, SparseCore 0:
  69.2 73.3 all-gather.5
  153.2 49.7 all-gather.3
  206.9 86.2 reduce-scatter.1
where the time goes:
time: 353 us; the launch traced here: 350 us
  waiting for transfers between devices  127 us (36%)
  matrix products  122 us (35%)
  blocking collectives  35.1 us (10%)
  local copies, waits for them, and re-layouts  29.2 us (8%)
  other arithmetic  17.1 us (5%)
  between operations  14.1 us (4%)
  starting transfers between devices  4.44 us (1%)
    all_gather x1, waiting for transfers between devices, total_of_pieces(): pieces = lax.all_gather(shard, axis)  72.4 us
    psum x5, blocking collectives, by_axis(): return functools.reduce(lax.psum, axes, shard)  35.1 us
    all_gather x1, waiting for transfers between devices, prefix(): pieces = lax.all_gather(value, axis)  32.3 us
    dot_general x21, matrix products, cmul(): jnp.matmul(left_im, right_im, precision=highest)  27.2 us
    dot_general x21, matrix products, cmul(): jnp.matmul(left_im, right_re, precision=highest)  27.1 us
    dot_general x21, matrix products, cmul(): jnp.matmul(left_re, right_re, precision=highest)  27 us
    dot_general x21, matrix products, cmul(): jnp.matmul(left_re, right_im, precision=highest)  27 us
    ppermute x1, waiting for transfers between devices, from_behind(): return lax.ppermute(block, axis, route)  22.4 us
  transfers between devices with their start and end apart: 4, of which 3 were waited for; matrix products, arithmetic and copies ran while one was open for 33% of the time, Pallas kernels for 0%

commit v1 on v0

v1 whole, which is shorter than its diff:
```python
import functools

import jax
import jax.numpy as jnp
from jax import lax
from jax.experimental import pallas as pl
from jax.experimental.pallas import tpu as pltpu
from jax.sharding import PartitionSpec as P

MESH = pl.DeviceIdType.MESH
F32 = jnp.float32
BF16 = jnp.bfloat16


def split(value):
    high = value.astype(BF16)
    low = (value - high.astype(F32)).astype(BF16)
    return high, low


def dot(left, right):
    return jnp.dot(left, right, preferred_element_type=F32)


def dot3(left, right_high, right_low):
    left_high, left_low = split(left)
    return dot(left_high, right_high) + (dot(left_high, right_low) + dot(left_low, right_high))


def cmul(left, right_re, right_im):
    rows = left.shape[0] // 2
    by_re = dot3(left, *split(right_re))
    by_im = dot3(left, *split(right_im))
    return by_re[:rows] - by_im[rows:], by_im[:rows] + by_re[rows:]


def kernel(
    ka, ga, coeffs, proj, deriv, shift, atoms, transport, forces,
    own, following, moved, lhs, rhs, part, arrived, mpart, mrows, erow, efull,
    xfull, tin, trow, tfull, fka, fga,
    load_sem, rhs_sem, nb_send, nb_recv, rs_send, rs_recv, m_send, m_recv, e_send, e_recv,
    t_send, t_recv, g_send, g_recv, f_send, f_recv, h_send, h_recv, out_sem,
):
    nb = own.shape[1]
    half = own.shape[0] // 2
    cols = part.shape[2] // 2
    rows = nb // ga
    k = lax.axis_index("ka")
    g = lax.axis_index("ga")

    def ga_at(offset):
        return lax.rem(g + offset, ga)

    def ka_at(offset):
        return lax.rem(k + offset, ka)

    own_load = pltpu.make_async_copy(coeffs, own, load_sem.at[0])
    own_load.start()

    def rhs_loads(i):
        target = ga_at(1 + i)
        slot = lax.rem(i, 3)
        at = pl.ds(pl.multiple_of(target * cols, cols), cols)
        return (
            pltpu.make_async_copy(proj.at[:, :, at], rhs.at[slot, :, :, pl.ds(0, cols)], rhs_sem.at[slot, 0]),
            pltpu.make_async_copy(deriv.at[:, :, at], rhs.at[slot, :, :, pl.ds(cols, cols)], rhs_sem.at[slot, 1]),
        )

    for i in range(2):
        for copy in rhs_loads(i):
            copy.start()

    barrier = pltpu.get_barrier_semaphore()
    for offset in range(1, ga):
        pl.semaphore_signal(barrier, inc=1, device_id={"ka": k, "ga": ga_at(offset)}, device_id_type=MESH)
    for offset in range(1, ka):
        pl.semaphore_signal(barrier, inc=1, device_id={"ka": ka_at(offset), "ga": g}, device_id_type=MESH)
    pl.semaphore_wait(barrier, ga + ka - 2)

    own_load.wait()
    neighbour = pltpu.make_async_remote_copy(
        src_ref=own, dst_ref=following, send_sem=nb_send, recv_sem=nb_recv,
        device_id={"ka": ka_at(ka - 1), "ga": g}, device_id_type=MESH)
    neighbour.start()

    for at in range(0, half, 384):
        width = min(384, half - at)
        re = own[at:at + width, :].T
        im = own[half + at:half + at + width, :].T
        lhs[0:nb, at:at + width] = re
        lhs[0:nb, half + at:half + at + width] = im
        lhs[nb:2 * nb, at:at + width] = im
        lhs[nb:2 * nb, half + at:half + at + width] = -re

    def rs_copy(i):
        return pltpu.make_async_remote_copy(
            src_ref=part.at[i], dst_ref=arrived.at[i], send_sem=rs_send.at[i], recv_sem=rs_recv.at[i],
            device_id={"ka": k, "ga": ga_at(1 + i)}, device_id_type=MESH)

    def project(i, carry):
        for copy in rhs_loads(i):
            copy.wait()

        @pl.when(i + 2 < ga)
        def _():
            for copy in rhs_loads(i + 2):
                copy.start()

        part[i] = dot(lhs[...], rhs[lax.rem(i, 3)].reshape(2 * half, 2 * cols))

        @pl.when(i < ga - 1)
        def _():
            rs_copy(i).start()

        return carry

    lax.fori_loop(0, ga, project, 0)

    neighbour.wait_recv()

    @pl.when(k == ka - 1)
    def _():
        lanes = lax.broadcasted_iota(jnp.int32, (128, 128), 1).astype(F32)
        base = (g * half).astype(F32)

        def permute(b, carry):
            blocks = []
            for s in range(3):
                line = shift[pl.ds(b * 3 + s, 1), :].astype(F32) - base
                column = jnp.broadcast_to(line, (128, 128)).T
                blocks.append(jnp.concatenate(
                    [jnp.where(column == lanes + 128.0 * h, 1.0, 0.0).astype(BF16) for h in range(half // 128)], axis=1))
            chosen = jnp.concatenate(blocks, axis=0)
            at = pl.multiple_of(b * 384, 384)
            moved[pl.ds(at, 384), :] = dot(chosen, following[0:half, :]).astype(BF16)
            moved[pl.ds(half + at, 384), :] = dot(chosen, following[half:2 * half, :]).astype(BF16)
            return carry

        lax.fori_loop(0, half // 384, permute, 0)
        following[...] = moved[...]

    mpart[...] = dot(lhs[...], following[...]).reshape(2, nb, nb)

    def m_copy(i):
        at = pl.ds(pl.multiple_of(ga_at(1 + i) * rows, rows), rows)
        return pltpu.make_async_remote_copy(
            src_ref=mpart.at[:, at, :], dst_ref=mrows.at[i], send_sem=m_send.at[i], recv_sem=m_recv.at[i],
            device_id={"ka": k, "ga": ga_at(1 + i)}, device_id_type=MESH)

    for i in range(ga - 1):
        m_copy(i).start()
    mine = pl.ds(pl.multiple_of(g * rows, rows), rows)
    total = mpart[:, mine, :]
    for i in range(ga - 1):
        m_copy(i).wait_recv()
        total = total + mrows[i]
    row_at = lax.broadcasted_iota(jnp.int32, (rows, nb), 0) + g * rows
    col_at = lax.broadcasted_iota(jnp.int32, (rows, nb), 1)
    erow[0] = jnp.where(row_at == col_at, 1.0, 0.0) - total[0]
    erow[1] = total[1]

    def spread(i, source, target, send, recv):
        return pltpu.make_async_remote_copy(
            src_ref=source, dst_ref=target.at[:, mine, :], send_sem=send.at[i], recv_sem=recv.at[i],
            device_id={"ka": k, "ga": ga_at(1 + i)}, device_id_type=MESH)

    for i in range(ga - 1):
        spread(i, erow, efull, e_send, e_recv).start()
    efull[:, mine, :] = erow[...]
    for i in range(ga - 1):
        spread(i, erow, efull, e_send, e_recv).wait_recv()

    e_re, e_im = efull[0], efull[1]
    both = efull[...].reshape(2 * nb, nb)
    sq_re, sq_im = cmul(both, e_re, e_im)
    eye = jnp.where(
        lax.broadcasted_iota(jnp.int32, (nb, nb), 0) == lax.broadcasted_iota(jnp.int32, (nb, nb), 1), 1.0, 0.0)
    cu_re, cu_im = cmul(both, sq_re, sq_im)
    xfull[0] = eye + (e_re + (sq_re + cu_re))
    xfull[1] = e_im + (sq_im + cu_im)

    onward = pltpu.make_async_remote_copy(
        src_ref=trow, dst_ref=tin, send_sem=t_send, recv_sem=t_recv,
        device_id={"ka": ka_at(1), "ga": g}, device_id_type=MESH)

    @pl.when(k == 0)
    def _():
        trow[...] = xfull[:, mine, :]

    @pl.when(k > 0)
    def _():
        onward.wait_recv()
        re, im = cmul(tin[...].reshape(2 * rows, nb), xfull[0], xfull[1])
        trow[0] = re
        trow[1] = im

    @pl.when(k < ka - 1)
    def _():
        onward.start()

    for i in range(ga - 1):
        spread(i, trow, tfull, g_send, g_recv).start()
    tfull[:, mine, :] = trow[...]

    whole = part[ga - 1]
    for i in range(ga - 1):
        rs_copy(i).wait_recv()
        whole = whole + arrived[i]
    b_both = jnp.concatenate([whole[0:nb, 0:cols].T, whole[nb:2 * nb, 0:cols].T], axis=0)
    d_re = whole[0:nb, cols:2 * cols].T
    d_im = whole[nb:2 * nb, cols:2 * cols].T
    atom_column = jnp.broadcast_to(atoms[pl.ds(g, 1), :].astype(F32), (cols, 128)).T

    for i in range(ga - 1):
        spread(i, trow, tfull, g_send, g_recv).wait_recv()
    out_copy = pltpu.make_async_copy(tfull, transport, out_sem)
    out_copy.start()
    w_re, w_im = cmul(b_both, tfull[0], tfull[1])
    per_proj = jnp.sum(d_re * w_im - d_im * w_re, axis=1, keepdims=True) * (1.0 / ka)
    atom_ids = lax.broadcasted_iota(jnp.int32, (cols, 128), 1).astype(F32)
    force = jnp.sum(jnp.where(atom_column == atom_ids, per_proj, 0.0), axis=0, keepdims=True)
    fka[k] = jnp.broadcast_to(force, (8, 128))

    def along_ka(i):
        return pltpu.make_async_remote_copy(
            src_ref=fka.at[k], dst_ref=fka.at[k], send_sem=f_send.at[i], recv_sem=f_recv.at[i],
            device_id={"ka": ka_at(1 + i), "ga": g}, device_id_type=MESH)

    def along_ga(i):
        return pltpu.make_async_remote_copy(
            src_ref=fga.at[g], dst_ref=fga.at[g], send_sem=h_send.at[i], recv_sem=h_recv.at[i],
            device_id={"ka": k, "ga": ga_at(1 + i)}, device_id_type=MESH)

    for i in range(ka - 1):
        along_ka(i).start()
    for i in range(ka - 1):
        along_ka(i).wait_recv()
    fga[g] = jnp.sum(fka[...], axis=0)
    for i in range(ga - 1):
        along_ga(i).start()
    for i in range(ga - 1):
        along_ga(i).wait_recv()
    forces[...] = jnp.sum(fga[...], axis=0)[0:1]

    neighbour.wait_send()
    for i in range(ga - 1):
        rs_copy(i).wait_send()
        m_copy(i).wait_send()
        spread(i, erow, efull, e_send, e_recv).wait_send()
        spread(i, trow, tfull, g_send, g_recv).wait_send()
        along_ga(i).wait_send()
    for i in range(ka - 1):
        along_ka(i).wait_send()

    @pl.when(k < ka - 1)
    def _():
        onward.wait_send()

    out_copy.wait()


def local(ka, ga, coeffs, projectors, proj_deriv, shift_map, atom_of):
    _, _, half, nb = coeffs.shape
    np_ = projectors.shape[2]
    cols = np_ // ga
    rows = nb // ga
    anywhere = pl.BlockSpec(memory_space=pl.ANY)
    vmem = pl.BlockSpec(memory_space=pltpu.VMEM)
    dma = pltpu.SemaphoreType.DMA
    transport, forces = pl.pallas_call(
        functools.partial(kernel, ka, ga),
        out_shape=(jax.ShapeDtypeStruct((2, nb, nb), F32), jax.ShapeDtypeStruct((1, 128), F32)),
        in_specs=[anywhere, anywhere, anywhere, vmem, vmem],
        out_specs=(anywhere, vmem),
        scratch_shapes=[
            pltpu.VMEM((2 * half, nb), BF16),
            pltpu.VMEM((2 * half, nb), BF16),
            pltpu.VMEM((2 * half, nb), BF16),
            pltpu.VMEM((2 * nb, 2 * half), BF16),
            pltpu.VMEM((3, 2, half, 2 * cols), BF16),
            pltpu.VMEM((ga, 2 * nb, 2 * cols), F32),
            pltpu.VMEM((ga - 1, 2 * nb, 2 * cols), F32),
            pltpu.VMEM((2, nb, nb), F32),
            pltpu.VMEM((ga - 1, 2, rows, nb), F32),
            pltpu.VMEM((2, rows, nb), F32),
            pltpu.VMEM((2, nb, nb), F32),
            pltpu.VMEM((2, nb, nb), F32),
            pltpu.VMEM((2, rows, nb), F32),
            pltpu.VMEM((2, rows, nb), F32),
            pltpu.VMEM((2, nb, nb), F32),
            pltpu.VMEM((ka, 8, 128), F32),
            pltpu.VMEM((ga, 8, 128), F32),
            dma((1,)), dma((3, 2)), dma, dma, dma((ga - 1,)), dma((ga - 1,)), dma((ga - 1,)), dma((ga - 1,)),
            dma((ga - 1,)), dma((ga - 1,)), dma, dma, dma((ga - 1,)), dma((ga - 1,)),
            dma((ka - 1,)), dma((ka - 1,)), dma((ga - 1,)), dma((ga - 1,)), dma,
        ],
        compiler_params=pltpu.CompilerParams(
            collective_id=0, has_side_effects=True, vmem_limit_bytes=60 * 1024 * 1024),
        name="string",
    )(
        coeffs.reshape(2 * half, nb), projectors, proj_deriv,
        shift_map.reshape(half // 128, 128), atom_of.reshape(ga, cols),
    )
    return transport[None], forces.reshape(128)


def solution(mesh):
    in_specs = (P("ka", None, "ga", None), P(None, "ga", None), P(None, "ga", None), P("ga"), P())
    out_specs = (P("ka", None, None, None), P())
    body = functools.partial(local, mesh.shape["ka"], mesh.shape["ga"])
    return jax.shard_map(body, mesh=mesh, in_specs=in_specs, out_specs=out_specs, check_vma=False)
```

time: 353 us -> 156 us (0.44)
  Pallas kernels: 0 us -> 152 us
  waiting for transfers between devices: 127 us -> 0 us
  matrix products: 122 us -> 0 us
  blocking collectives: 35.1 us -> 0 us
  local copies, waits for them, and re-layouts: 29.2 us -> 2.97 us
  other arithmetic: 17.1 us -> 0 us
  between operations: 14.1 us -> 0.64 us
  starting transfers between devices: 4.44 us -> 0 us
    pallas_call x0 -> x1, Pallas kernels: none -> 152 us  [local(): pl.pallas_call(functools.partial(kernel, ka, ga), out_shape=(jax.ShapeDty...]
    dot_general x91 -> x0, matrix products: 122 us -> none  [the longest x21 27.2 us: cmul(): jnp.matmul(left_im, right_im, precision=highest)]
    all_gather x2 -> x0, waiting for transfers between devices: 105 us -> none  [the longest x1 72.4 us: total_of_pieces(): pieces = lax.all_gather(shard, axis)]
    psum x5 -> x0, blocking collectives: 35.1 us -> none  [by_axis(): return functools.reduce(lax.psum, axes, shard)]
    ppermute x1 -> x0, waiting for transfers between devices: 22.4 us -> none  [from_behind(): return lax.ppermute(block, axis, route)]
    unnamed x17 -> x2, local copies, waits for them, and re-layouts: 18.7 us -> 2.97 us
    gather x1 -> x0, local copies, waits for them, and re-layouts: 8.31 us -> none  [local(): arrived[:, local_map, :]]
    select_n x17 -> x0, other arithmetic: 5.6 us -> none  [the longest x1 3.66 us: local(): jnp.where(position == string_devices - 1, arrived[:, local_map, :], arrived)]
  transfers between devices with their start and end apart: 4 -> 0, of which waited for: 3 -> 0; matrix products, arithmetic and copies ran while one was open for 33% -> 0% of each run, Pallas kernels for 0% -> 0%
where the time goes in v1:
time: 156 us
  Pallas kernels  152 us (97%)
  local copies, waits for them, and re-layouts  2.97 us (2%)
    pallas_call x1, Pallas kernels, local(): pl.pallas_call(functools.partial(kernel, ka, ga), out_shape=(jax.ShapeDty...  152 us

profile of v1, /device:TPU:0, one launch (start us, length us, event | category | flops | bytes accessed | tf_op | source)
XLA Modules:
  0.0 156.0 jit_solution(17357928146958375442)
XLA Ops:
  0.6 152.4 %string.1 = (f32[2,256,256]{2,1,0:T(8,128)}, f32[1,128]{1,0:T(1,128)}) custom-call(bf16[3840,256]{1,0:T(8,128)(2,1)} %bitcast.5, bf16[2,1920,1024]{2,1,0:T(8,128)(2,1)} %proj.1, bf16[2,1920,1024]{2,1,0:T(8,128)(2,1)} %deriv.1, s32[15,128]{1,0:T(8,128)} %bitcast.7, s32[8,128]{1,0:T(8,128)} %bitcast.8), custom_call_target="tpu_custom_call" | custom-call | tf_op jit(solution)/shard_map/string/pallas_call | solution.py:270
  153.0 1.9 %copy.9 = f32[1,2,256,256]{3,2,1,0:T(8,128)} copy(f32[1,2,256,256]{3,2,1,0:T(8,128)} %bitcast.6) | data formatting | bytes 1048576
  154.9 1.1 copy.10

commit v2 on v1

v2 whole, which is shorter than its diff:
```python
import functools

import jax
import jax.numpy as jnp
from jax import lax
from jax.experimental import pallas as pl
from jax.experimental.pallas import tpu as pltpu
from jax.sharding import PartitionSpec as P

MESH = pl.DeviceIdType.MESH
F32 = jnp.float32
BF16 = jnp.bfloat16
I16 = jnp.int16
BANDS = 64
EARLY = 2


def split(value):
    high = value.astype(BF16)
    low = (value - high.astype(F32)).astype(BF16)
    return high, low


def dot(left, right):
    return jnp.dot(left, right, preferred_element_type=F32)


def dot3(left, right_high, right_low):
    left_high, left_low = split(left)
    return dot(left_high, right_high) + (dot(left_high, right_low) + dot(left_low, right_high))


def join(by_re, by_im):
    rows = by_re.shape[0] // 2
    return by_re[:rows] - by_im[rows:], by_im[:rows] + by_re[rows:]


def cmul(left, right_re, right_im):
    return join(dot3(left, *split(right_re)), dot3(left, *split(right_im)))


def kernel(
    ka, ga, coeffs, proj, deriv, shift, atoms, transport, forces,
    own, moved, lhs, nbt, rhs, part, pieces, scales, in_pieces, in_scales, mpart, mrows, erow, efull,
    xfull, xmate, qhigh, qlow, tin, trow, tfull, fka, fga,
    load_sem, rhs_sem, nb_send, nb_recv, p_send, p_recv, m_send, m_recv, e_send, e_recv,
    x_send, x_recv, t_send, t_recv, g_send, g_recv, h_send, f_send, f_recv, l_send, l_recv, out_sem, ready_sem,
):
    phases = []

    def phase(name):
        if phases:
            phases.pop().__exit__(None, None, None)
        if name:
            phases.append(jax.named_scope(name))
            phases[-1].__enter__()

    phase("start")
    nb = own.shape[1]
    half = own.shape[0] // 2
    cols = part.shape[1] // 2
    rows = nb // ga
    blocks = nb // BANDS
    brows = BANDS // ga
    k = lax.axis_index("ka")
    g = lax.axis_index("ga")
    odd = lax.rem(k, 2)
    mate = k + 1 - 2 * odd

    def ga_at(offset):
        return lax.rem(g + offset, ga)

    def ka_at(offset):
        return lax.rem(k + offset, ka)

    def remote(source, target, send, recv, to_k, to_g):
        return pltpu.make_async_remote_copy(
            src_ref=source, dst_ref=target, send_sem=send, recv_sem=recv,
            device_id={"ka": to_k, "ga": to_g}, device_id_type=MESH)

    own_load = pltpu.make_async_copy(coeffs, own, load_sem)
    own_load.start()

    def rhs_loads(i):
        target = ga_at(1 + i)
        slot = lax.rem(i, 3)
        at = pl.ds(pl.multiple_of(target * cols, cols), cols)
        return (
            pltpu.make_async_copy(proj.at[:, :, at], rhs.at[slot, :, :, pl.ds(0, cols)], rhs_sem.at[slot, 0]),
            pltpu.make_async_copy(deriv.at[:, :, at], rhs.at[slot, :, :, pl.ds(cols, cols)], rhs_sem.at[slot, 1]),
        )

    for i in range(2):
        for copy in rhs_loads(i):
            copy.start()

    phase("barrier")
    barrier = pltpu.get_barrier_semaphore()
    for offset in range(1, ga):
        pl.semaphore_signal(barrier, inc=1, device_id={"ka": k, "ga": ga_at(offset)}, device_id_type=MESH)
    for offset in range(ga):
        pl.semaphore_signal(barrier, inc=1, device_id={"ka": mate, "ga": ga_at(offset)}, device_id_type=MESH)
    for offset in range(1, ka - 1):
        other = lax.rem(lax.max(k, mate) + offset, ka)
        pl.semaphore_signal(barrier, inc=1, device_id={"ka": other, "ga": g}, device_id_type=MESH)
    pl.semaphore_wait(barrier, 2 * ga + ka - 3)

    phase("load")
    own_load.wait()

    phase("lhs")
    for at in range(0, half, 384):
        width = min(384, half - at)
        re = own[at:at + width, :].T
        im = own[half + at:half + at + width, :].T
        lhs[0:nb, at:at + width] = re
        lhs[0:nb, half + at:half + at + width] = im
        lhs[nb:2 * nb, at:at + width] = im
        lhs[nb:2 * nb, half + at:half + at + width] = -re

    def nb_copy(b):
        return remote(lhs.at[pl.ds(b * BANDS, BANDS)], nbt.at[b], nb_send.at[b], nb_recv.at[b], ka_at(ka - 1), g)

    for b in range(blocks):
        nb_copy(b).start()

    def piece_copies(i):
        return (
            remote(pieces.at[i], in_pieces.at[i], p_send.at[i, 0], p_recv.at[i, 0], k, ga_at(1 + i)),
            remote(scales.at[i], in_scales.at[i], p_send.at[i, 1], p_recv.at[i, 1], k, ga_at(1 + i)),
        )

    def project(i, carry):
        for copy in rhs_loads(i):
            copy.wait()

        @pl.when(i + 2 < ga)
        def _():
            for copy in rhs_loads(i + 2):
                copy.start()

        part[...] = dot(lhs[...], rhs[lax.rem(i, 3)].reshape(2 * half, 2 * cols))

        @pl.when(i < ga - 1)
        def _():
            values = part[...]
            top = jnp.maximum(jnp.max(jnp.abs(values), axis=0, keepdims=True), 1e-30)
            pieces[i] = jnp.round(values * (32767.0 / top)).astype(jnp.int32).astype(I16)
            scales[i] = jnp.broadcast_to(top * (1.0 / 32767.0), (8, 2 * cols))

        @pl.when(i < EARLY)
        def _():
            for copy in piece_copies(i):
                copy.start()

        return carry

    def m_copy(b, i):
        target = ga_at(1 + i)
        at = pl.ds(pl.multiple_of(target * brows, brows), brows)
        return remote(mpart.at[b, :, at, :], mrows.at[b, i], m_send.at[b, i], m_recv.at[b, i], k, target)

    def intersect(b):
        phase(f"nb_wait{b}")
        nb_copy(b).wait_recv()
        phase(f"m_dot{b}")
        block = nbt[b]
        swapped = jnp.concatenate([block[:, half:], -block[:, :half]], axis=1)
        mpart[b] = dot(jnp.concatenate([block, swapped], axis=0), own[...]).reshape(2, BANDS, nb)
        for i in range(ga - 1):
            m_copy(b, i).start()

    def e_copy(b, i):
        at = pl.ds(pl.multiple_of(b * BANDS + g * brows, brows), brows)
        return remote(erow.at[b], efull.at[:, at, :], e_send.at[b, i], e_recv.at[b, i], k, ga_at(1 + i))

    def settle(b):
        phase(f"m_rs{b}")
        total = mpart[b, :, pl.ds(pl.multiple_of(g * brows, brows), brows), :]
        for i in range(ga - 1):
            m_copy(b, i).wait_recv()
            total = total + mrows[b, i]
        first = b * BANDS + g * brows
        row_at = lax.broadcasted_iota(jnp.int32, (brows, nb), 0) + first
        col_at = lax.broadcasted_iota(jnp.int32, (brows, nb), 1)
        erow[b, 0] = jnp.where(row_at == col_at, 1.0, 0.0) - total[0]
        erow[b, 1] = -total[1]
        for i in range(ga - 1):
            e_copy(b, i).start()
        efull[:, pl.ds(pl.multiple_of(first, brows), brows), :] = erow[b]

    phase("project0")
    lax.fori_loop(0, 4, project, 0)

    phase("permute")

    @pl.when(k == ka - 1)
    def _():
        wanted = shift[...] - g * half

        def permute(b, carry):
            at = pl.multiple_of(b * 384, 384)
            index = lax.broadcasted_iota(jnp.int32, (384, half), 0) + at
            chosen = jnp.where(wanted == index, 1.0, 0.0).astype(BF16)
            moved[pl.ds(at, 384), :] = dot(chosen, own[0:half, :]).astype(BF16)
            moved[pl.ds(half + at, 384), :] = dot(chosen, own[half:2 * half, :]).astype(BF16)
            return carry

        lax.fori_loop(0, half // 384, permute, 0)
        own[...] = moved[...]

    intersect(0)
    phase("project1")
    lax.fori_loop(4, 6, project, 0)
    intersect(1)
    settle(0)
    phase("project2")
    lax.fori_loop(6, ga, project, 0)
    intersect(2)
    settle(1)
    intersect(3)
    settle(2)
    settle(3)

    phase("token")

    @pl.when(odd == 1)
    def _():
        pl.semaphore_signal(ready_sem, inc=1, device_id={"ka": mate, "ga": g}, device_id_type=MESH)

    @pl.when(odd == 0)
    def _():
        pl.semaphore_wait(ready_sem, 1)

    for i in range(EARLY, ga - 1):
        for copy in piece_copies(i):
            copy.start()

    phase("e_ag")
    for b in range(blocks):
        for i in range(ga - 1):
            e_copy(b, i).wait_recv()

    phase("newton")
    e_re, e_im = efull[0], efull[1]
    both = efull[...].reshape(2 * nb, nb)
    sq_re, sq_im = cmul(both, e_re, e_im)
    eye = jnp.where(
        lax.broadcasted_iota(jnp.int32, (nb, nb), 0) == lax.broadcasted_iota(jnp.int32, (nb, nb), 1), 1.0, 0.0)
    cu_re, cu_im = cmul(both, sq_re, sq_im)
    xfull[0] = (eye + (e_re + (sq_re + cu_re))).T
    xfull[1] = (e_im + (sq_im + cu_im)).T

    phase("chain")
    mine = pl.ds(pl.multiple_of(g * rows, rows), rows)
    x_copy = remote(xfull, xmate, x_send, x_recv, mate, g)
    onward = remote(trow.at[1], tin, t_send, t_recv, ka_at(2), g)

    def same_copy(i):
        return remote(trow.at[1], tfull.at[:, mine, :], g_send.at[i], g_recv.at[i], k, ga_at(i))

    def mate_copy(i):
        return remote(trow.at[0], tfull.at[:, mine, :], h_send.at[i], g_recv.at[i], mate, ga_at(i))

    @pl.when(odd == 0)
    def _():
        x_copy.start()

    @pl.when(odd == 1)
    def _():
        phase("x_wait")
        x_copy.wait_recv()

        def keep(re, im):
            high, low = split(re)
            qhigh[:, 0:nb] = high
            qlow[:, 0:nb] = low
            high, low = split(im)
            qhigh[:, nb:2 * nb] = high
            qlow[:, nb:2 * nb] = low

        def step(left, high, low):
            out = dot3(left, high, low)
            return join(out[:, 0:nb], out[:, nb:2 * nb])

        phase("q")

        @pl.when(k == 1)
        def _():
            keep(xfull[0], xfull[1])
            tin[...] = xmate[:, mine, :]

        @pl.when(k > 1)
        def _():
            keep(*cmul(xmate[...].reshape(2 * nb, nb), xfull[0], xfull[1]))
            phase("t_in")
            onward.wait_recv()

        phase("t_step")
        left = tin[...].reshape(2 * rows, nb)
        re, im = step(left, qhigh[...], qlow[...])
        trow[1, 0] = re
        trow[1, 1] = im

        @pl.when(k < ka - 1)
        def _():
            onward.start()

        for i in range(1, ga):
            same_copy(i).start()
        tfull[:, mine, :] = trow[1]

        phase("t_mate")

        @pl.when(k == 1)
        def _():
            trow[0] = tin[...]

        @pl.when(k > 1)
        def _():
            re, im = cmul(left, xmate[0], xmate[1])
            trow[0, 0] = re
            trow[0, 1] = im

        for i in range(ga):
            mate_copy(i).start()

    phase("p_wait")
    for i in range(ga - 1):
        for copy in piece_copies(i):
            copy.wait_recv()
    phase("p_sum")
    whole = part[...]
    for i in range(ga - 1):
        whole = whole + in_pieces[i].astype(jnp.int32).astype(F32) * in_scales[i, 0:1, :]
    b_both = jnp.concatenate([whole[0:nb, 0:cols].T, whole[nb:2 * nb, 0:cols].T], axis=0)
    d_re = whole[0:nb, cols:2 * cols].T
    d_im = whole[nb:2 * nb, cols:2 * cols].T
    atom_column = jnp.broadcast_to(atoms[pl.ds(g, 1), :].astype(F32), (cols, 128)).T

    phase("t_ag")
    for i in range(1, ga):
        same_copy(i).wait_recv()

    @pl.when(odd == 0)
    def _():
        mate_copy(0).wait_recv()

    phase("w")
    out_copy = pltpu.make_async_copy(tfull, transport, out_sem)
    out_copy.start()
    w_re, w_im = cmul(b_both, tfull[0], tfull[1])
    per_proj = jnp.sum(d_re * w_im - d_im * w_re, axis=1, keepdims=True) * (1.0 / ka)
    atom_ids = lax.broadcasted_iota(jnp.int32, (cols, 128), 1).astype(F32)
    force = jnp.sum(jnp.where(atom_column == atom_ids, per_proj, 0.0), axis=0, keepdims=True)
    fka[k] = jnp.broadcast_to(force, (8, 128))

    def along_ka(i):
        return remote(fka.at[k], fka.at[k], f_send.at[i], f_recv.at[i], ka_at(1 + i), g)

    def along_ga(i):
        return remote(fga.at[g], fga.at[g], l_send.at[i], l_recv.at[i], k, ga_at(1 + i))

    phase("f_ka")
    for i in range(ka - 1):
        along_ka(i).start()
    for i in range(ka - 1):
        along_ka(i).wait_recv()
    phase("f_ga")
    fga[g] = jnp.sum(fka[...], axis=0)
    for i in range(ga - 1):
        along_ga(i).start()
    for i in range(ga - 1):
        along_ga(i).wait_recv()
    forces[...] = jnp.sum(fga[...], axis=0)[0:1]

    phase("drain")
    for b in range(blocks):
        nb_copy(b).wait_send()
        for i in range(ga - 1):
            m_copy(b, i).wait_send()
            e_copy(b, i).wait_send()
    for i in range(ga - 1):
        for copy in piece_copies(i):
            copy.wait_send()
        along_ga(i).wait_send()
    for i in range(ka - 1):
        along_ka(i).wait_send()

    @pl.when(odd == 0)
    def _():
        x_copy.wait_send()

    @pl.when(odd == 1)
    def _():
        for i in range(1, ga):
            same_copy(i).wait_send()
        for i in range(ga):
            mate_copy(i).wait_send()

        @pl.when(k < ka - 1)
        def _():
            onward.wait_send()

    out_copy.wait()
    phase(None)


def local(ka, ga, coeffs, projectors, proj_deriv, shift_map, atom_of):
    _, _, half, nb = coeffs.shape
    np_ = projectors.shape[2]
    cols = np_ // ga
    rows = nb // ga
    blocks = nb // BANDS
    brows = BANDS // ga
    anywhere = pl.BlockSpec(memory_space=pl.ANY)
    vmem = pl.BlockSpec(memory_space=pltpu.VMEM)
    dma = pltpu.SemaphoreType.DMA
    transport, forces = pl.pallas_call(
        functools.partial(kernel, ka, ga),
        out_shape=(jax.ShapeDtypeStruct((2, nb, nb), F32), jax.ShapeDtypeStruct((1, 128), F32)),
        in_specs=[anywhere, anywhere, anywhere, vmem, vmem],
        out_specs=(anywhere, vmem),
        scratch_shapes=[
            pltpu.VMEM((2 * half, nb), BF16),
            pltpu.VMEM((2 * half, nb), BF16),
            pltpu.VMEM((2 * nb, 2 * half), BF16),
            pltpu.VMEM((blocks, BANDS, 2 * half), BF16),
            pltpu.VMEM((3, 2, half, 2 * cols), BF16),
            pltpu.VMEM((2 * nb, 2 * cols), F32),
            pltpu.VMEM((ga - 1, 2 * nb, 2 * cols), I16),
            pltpu.VMEM((ga - 1, 8, 2 * cols), F32),
            pltpu.VMEM((ga - 1, 2 * nb, 2 * cols), I16),
            pltpu.VMEM((ga - 1, 8, 2 * cols), F32),
            pltpu.VMEM((blocks, 2, BANDS, nb), F32),
            pltpu.VMEM((blocks, ga - 1, 2, brows, nb), F32),
            pltpu.VMEM((blocks, 2, brows, nb), F32),
            pltpu.VMEM((2, nb, nb), F32),
            pltpu.VMEM((2, nb, nb), F32),
            pltpu.VMEM((2, nb, nb), F32),
            pltpu.VMEM((nb, 2 * nb), BF16),
            pltpu.VMEM((nb, 2 * nb), BF16),
            pltpu.VMEM((2, rows, nb), F32),
            pltpu.VMEM((2, 2, rows, nb), F32),
            pltpu.VMEM((2, nb, nb), F32),
            pltpu.VMEM((ka, 8, 128), F32),
            pltpu.VMEM((ga, 8, 128), F32),
            dma, dma((3, 2)), dma((blocks,)), dma((blocks,)), dma((ga - 1, 2)), dma((ga - 1, 2)),
            dma((blocks, ga - 1)), dma((blocks, ga - 1)), dma((blocks, ga - 1)), dma((blocks, ga - 1)),
            dma, dma, dma, dma, dma((ga,)), dma((ga,)), dma((ga,)),
            dma((ka - 1,)), dma((ka - 1,)), dma((ga - 1,)), dma((ga - 1,)), dma,
            pltpu.SemaphoreType.REGULAR,
        ],
        compiler_params=pltpu.CompilerParams(
            collective_id=0, has_side_effects=True, vmem_limit_bytes=60 * 1024 * 1024),
        name="string",
    )(
        coeffs.reshape(2 * half, nb), projectors, proj_deriv,
        shift_map.reshape(1, half), atom_of.reshape(ga, cols),
    )
    return transport[None], forces.reshape(128)


def solution(mesh):
    in_specs = (P("ka", None, "ga", None), P(None, "ga", None), P(None, "ga", None), P("ga"), P())
    out_specs = (P("ka", None, None, None), P())
    body = functools.partial(local, mesh.shape["ka"], mesh.shape["ga"])
    return jax.shard_map(body, mesh=mesh, in_specs=in_specs, out_specs=out_specs, check_vma=False)
```

time: 156 us -> 111 us (0.71)
  Pallas kernels: 152 us -> 106 us
    pallas_call x1, Pallas kernels: 152 us -> 106 us  [local(): pl.pallas_call(functools.partial(kernel, ka, ga), out_shape=(jax.ShapeDty...]
where the time goes in v2:
time: 111 us
  Pallas kernels  106 us (95%)
  local copies, waits for them, and re-layouts  4.27 us (4%)
    pallas_call x1, Pallas kernels, local(): pl.pallas_call(functools.partial(kernel, ka, ga), out_shape=(jax.ShapeDty...  106 us
    unnamed x2, local copies, waits for them, and re-layouts  2.97 us

profile of v2, /device:TPU:0, one launch (start us, length us, event | category | flops | bytes accessed | tf_op | source)
XLA Modules:
  0.0 110.8 jit_solution(18256048531242406102)
XLA Ops:
  0.6 1.3 %reshape.17.shift = s32[1,1920]{1,0:T(1,128)} reshape(s32[1920]{0:T(1024)} %param.8) | data formatting | bytes 15360 | tf_op jit(solution)/shard_map/reshape | solution.py:459
  1.9 105.9 %string.1 = (f32[2,256,256]{2,1,0:T(8,128)}, f32[1,128]{1,0:T(1,128)}) custom-call(bf16[3840,256]{1,0:T(8,128)(2,1)} %bitcast.4, bf16[2,1920,1024]{2,1,0:T(8,128)(2,1)} %proj.1, bf16[2,1920,1024]{2,1,0:T(8,128)(2,1)} %deriv.1, s32[1,1920]{1,0:T(1,128)} %reshape.17.shift, s32[8,128]{1,0:T(8,128)} %bitcast.6), custom_call_target="tpu_custom_call" | custom-call | tf_op jit(solution)/shard_map/string/pallas_call | solution.py:419
  107.8 1.9 %copy.9 = f32[1,2,256,256]{3,2,1,0:T(8,128)} copy(f32[1,2,256,256]{3,2,1,0:T(8,128)} %bitcast.5) | data formatting | bytes 1048576
  109.7 1.1 copy.10

commit v3 on v2

--- a/solution.py
+++ b/solution.py
@@ -12,7 +12,9 @@
 BF16 = jnp.bfloat16
 I16 = jnp.int16
 BANDS = 64
+SHARED = 640
 EARLY = 2
+LATE = 8
 
 
 def split(value):
@@ -41,9 +43,9 @@
 
 def kernel(
     ka, ga, coeffs, proj, deriv, shift, atoms, transport, forces,
-    own, moved, lhs, nbt, rhs, part, pieces, scales, in_pieces, in_scales, mpart, mrows, erow, efull,
+    own, moved, lhs, nbt, cnat, taken, taken_rows, taken_sum, taken_in, rhs, part, pieces, scales, in_pieces, in_scales, z_piece, z_scale, z_in, z_in_scale, mpart, mrows, erow, efull,
     xfull, xmate, qhigh, qlow, tin, trow, tfull, fka, fga,
-    load_sem, rhs_sem, nb_send, nb_recv, p_send, p_recv, m_send, m_recv, e_send, e_recv,
+    load_sem, rhs_sem, nb_send, nb_recv, z_send, z_recv, c_send, c_recv, a_send, a_recv, s_send, s_recv, p_send, p_recv, m_send, m_recv, e_send, e_recv,
     x_send, x_recv, t_send, t_recv, g_send, g_recv, h_send, f_send, f_recv, l_send, l_recv, out_sem, ready_sem,
 ):
     phases = []
@@ -58,14 +60,17 @@
     phase("start")
     nb = own.shape[1]
     half = own.shape[0] // 2
-    cols = part.shape[1] // 2
+    cols = part.shape[2] // 2
     rows = nb // ga
     blocks = nb // BANDS
     brows = BANDS // ga
+    kept = half - SHARED
     k = lax.axis_index("ka")
     g = lax.axis_index("ga")
     odd = lax.rem(k, 2)
     mate = k + 1 - 2 * odd
+    ring = ga // 2
+    ring_at, place = g // 2, lax.rem(g, 2)
 
     def ga_at(offset):
         return lax.rem(g + offset, ga)
@@ -81,8 +86,18 @@
     own_load = pltpu.make_async_copy(coeffs, own, load_sem)
     own_load.start()
 
+    def along_ring(step):
+        return lax.rem(ring_at + step, ring) * 2
+
+    def block_of(i):
+        last = i // 4
+        step = (1 - last) * (1 + 2 * lax.rem(i, 2)) + last * (6 - 2 * (i // 2))
+        other = (1 - last) * (1 - i // 2) + last * (1 - lax.rem(i, 2))
+        return step, other
+
     def rhs_loads(i):
-        target = ga_at(1 + i)
+        step, other = block_of(i)
+        target = along_ring(step) + place + other - 2 * place * other
         slot = lax.rem(i, 3)
         at = pl.ds(pl.multiple_of(target * cols, cols), cols)
         return (
@@ -118,85 +133,44 @@
         lhs[nb:2 * nb, at:at + width] = im
         lhs[nb:2 * nb, half + at:half + at + width] = -re
 
-    def nb_copy(b):
-        return remote(lhs.at[pl.ds(b * BANDS, BANDS)], nbt.at[b], nb_send.at[b], nb_recv.at[b], ka_at(ka - 1), g)
-
-    for b in range(blocks):
-        nb_copy(b).start()
-
-    def piece_copies(i):
-        return (
-            remote(pieces.at[i], in_pieces.at[i], p_send.at[i, 0], p_recv.at[i, 0], k, ga_at(1 + i)),
-            remote(scales.at[i], in_scales.at[i], p_send.at[i, 1], p_recv.at[i, 1], k, ga_at(1 + i)),
-        )
-
-    def project(i, carry):
-        for copy in rhs_loads(i):
-            copy.wait()
-
-        @pl.when(i + 2 < ga)
-        def _():
-            for copy in rhs_loads(i + 2):
-                copy.start()
-
-        part[...] = dot(lhs[...], rhs[lax.rem(i, 3)].reshape(2 * half, 2 * cols))
-
-        @pl.when(i < ga - 1)
-        def _():
-            values = part[...]
-            top = jnp.maximum(jnp.max(jnp.abs(values), axis=0, keepdims=True), 1e-30)
-            pieces[i] = jnp.round(values * (32767.0 / top)).astype(jnp.int32).astype(I16)
-            scales[i] = jnp.broadcast_to(top * (1.0 / 32767.0), (8, 2 * cols))
-
-        @pl.when(i < EARLY)
-        def _():
-            for copy in piece_copies(i):
-                copy.start()
-
-        return carry
-
-    def m_copy(b, i):
-        target = ga_at(1 + i)
-        at = pl.ds(pl.multiple_of(target * brows, brows), brows)
-        return remote(mpart.at[b, :, at, :], mrows.at[b, i], m_send.at[b, i], m_recv.at[b, i], k, target)
-
-    def intersect(b):
-        phase(f"nb_wait{b}")
-        nb_copy(b).wait_recv()
-        phase(f"m_dot{b}")
-        block = nbt[b]
-        swapped = jnp.concatenate([block[:, half:], -block[:, :half]], axis=1)
-        mpart[b] = dot(jnp.concatenate([block, swapped], axis=0), own[...]).reshape(2, BANDS, nb)
-        for i in range(ga - 1):
-            m_copy(b, i).start()
-
-    def e_copy(b, i):
-        at = pl.ds(pl.multiple_of(b * BANDS + g * brows, brows), brows)
-        return remote(erow.at[b], efull.at[:, at, :], e_send.at[b, i], e_recv.at[b, i], k, ga_at(1 + i))
-
-    def settle(b):
-        phase(f"m_rs{b}")
-        total = mpart[b, :, pl.ds(pl.multiple_of(g * brows, brows), brows), :]
-        for i in range(ga - 1):
-            m_copy(b, i).wait_recv()
-            total = total + mrows[b, i]
-        first = b * BANDS + g * brows
-        row_at = lax.broadcasted_iota(jnp.int32, (brows, nb), 0) + first
-        col_at = lax.broadcasted_iota(jnp.int32, (brows, nb), 1)
-        erow[b, 0] = jnp.where(row_at == col_at, 1.0, 0.0) - total[0]
-        erow[b, 1] = -total[1]
-        for i in range(ga - 1):
-            e_copy(b, i).start()
-        efull[:, pl.ds(pl.multiple_of(first, brows), brows), :] = erow[b]
-
-    phase("project0")
-    lax.fori_loop(0, 4, project, 0)
+    ranges = ((0, kept), (half, kept), (kept, SHARED), (half + kept, SHARED))
+
+    def nb_copy(b, r):
+        at = pl.ds(*ranges[r])
+        return remote(lhs.at[pl.ds(b * BANDS, BANDS), at], nbt.at[b, :, at], nb_send.at[b, r], nb_recv.at[b, r],
+                      ka_at(ka - 1), g)
+
+    plane = ka // 2
+    turn = lax.rem(k, plane) == 0
+
+    def nb_start(b):
+        for r in range(2):
+            nb_copy(b, r).start()
+
+    def nb_turn(b):
+        @pl.when(turn)
+        def _():
+            nb_start(b)
+
+    nb_start(0)
+    nb_start(1)
+
+    @pl.when(jnp.logical_not(turn))
+    def _():
+        nb_start(2)
+        nb_start(3)
+
+    @pl.when(odd == 1)
+    def _():
+        for b in range(blocks):
+            for r in range(2, 4):
+                nb_copy(b, r).start()
 
     phase("permute")
 
     @pl.when(k == ka - 1)
     def _():
-        wanted = shift[...] - g * half
+        wanted = jnp.concatenate([shift[r:r + 1, :] for r in range(half // 128)], axis=1) - g * half
 
         def permute(b, carry):
             at = pl.multiple_of(b * 384, 384)
@@ -209,37 +183,177 @@
         lax.fori_loop(0, half // 384, permute, 0)
         own[...] = moved[...]
 
+    def c_copy(r):
+        return remote(own.at[pl.ds(kept + r * half, SHARED)], cnat.at[r], c_send.at[r], c_recv.at[r], ka_at(1), g)
+
+    @pl.when(odd == 1)
+    def _():
+        for r in range(2):
+            c_copy(r).start()
+
+    def piece_copies(i):
+        return (
+            remote(pieces.at[i], in_pieces.at[i], p_send.at[i, 0], p_recv.at[i, 0], k, along_ring(block_of(i)[0]) + place),
+            remote(scales.at[i], in_scales.at[i], p_send.at[i, 1], p_recv.at[i, 1], k, along_ring(block_of(i)[0]) + place),
+        )
+
+    def coded(values):
+        top = jnp.maximum(jnp.max(jnp.abs(values), axis=0, keepdims=True), 1e-30)
+        code = jnp.round(values * (32767.0 / top)).astype(jnp.int32).astype(I16)
+        return code, jnp.broadcast_to(top * (1.0 / 32767.0), (8, 2 * cols))
+
+    def decoded(code, scale):
+        return code.astype(jnp.int32).astype(F32) * scale[0:1, :]
+
+    def project(i, carry):
+        for copy in rhs_loads(i):
+            copy.wait()
+
+        @pl.when(i + 2 < ga)
+        def _():
+            for copy in rhs_loads(i + 2):
+                copy.start()
+
+        part[i] = dot(lhs[...], rhs[lax.rem(i, 3)].reshape(2 * half, 2 * cols))
+
+        @pl.when(i < ga - 2)
+        def _():
+            code, scale = coded(part[i])
+            pieces[i] = code
+            scales[i] = scale
+
+        @pl.when(i < EARLY)
+        def _():
+            for copy in piece_copies(i):
+                copy.start()
+
+        return carry
+
+    def m_copy(b, i):
+        target = ga_at(1 + i)
+        at = pl.ds(pl.multiple_of(target * brows, brows), brows)
+        return remote(mpart.at[b, :, at, :], mrows.at[b, i], m_send.at[b, i], m_recv.at[b, i], k, target)
+
+    def intersect(b):
+        phase(f"nb_wait{b}")
+
+        def over(count):
+            re, im = nbt[b, :, 0:count], nbt[b, :, half:half + count]
+            by_re = dot(jnp.concatenate([re, im], axis=0), own[0:count, :])
+            by_im = dot(jnp.concatenate([im, -re], axis=0), own[half:half + count, :])
+            mpart[b] = (by_re + by_im).reshape(2, BANDS, nb)
+
+        for r in range(2):
+            nb_copy(b, r).wait_recv()
+
+        @pl.when(odd == 1)
+        def _():
+            over(kept)
+
+        @pl.when(odd == 0)
+        def _():
+            for r in range(2, 4):
+                nb_copy(b, r).wait_recv()
+            over(half)
+
+        phase(f"m_dot{b}")
+        for i in range(ga - 1):
+            m_copy(b, i).start()
+
+    def a_copy(i):
+        at = pl.ds(pl.multiple_of(ga_at(1 + i) * brows, brows), brows)
+        return remote(taken.at[:, :, at, :], taken_rows.at[i], a_send.at[i], a_recv.at[i], k, ga_at(1 + i))
+
+    s_copy = remote(taken_sum, taken_in, s_send, s_recv, ka_at(ka - 1), g)
+
+    def take():
+        for r in range(2):
+            c_copy(r).wait_recv()
+        out = dot(lhs[:, kept:half], cnat[0]) + dot(lhs[:, half + kept:2 * half], cnat[1])
+        taken[...] = out.reshape(2, blocks, BANDS, nb)
+        for i in range(ga - 1):
+            a_copy(i).start()
+
+    def give_back():
+        out = taken[:, :, pl.ds(pl.multiple_of(g * brows, brows), brows), :]
+        for i in range(ga - 1):
+            a_copy(i).wait_recv()
+            out = out + taken_rows[i]
+        taken_sum[...] = out
+        s_copy.start()
+
+    even = jnp.logical_and(odd == 0, k > 0)
+
+    def e_copy(b, i):
+        at = pl.ds(pl.multiple_of(b * BANDS + g * brows, brows), brows)
+        return remote(erow.at[b], efull.at[:, at, :], e_send.at[b, i], e_recv.at[b, i], k, ga_at(1 + i))
+
+    def settle(b):
+        phase(f"m_rs{b}")
+        total = mpart[b, :, pl.ds(pl.multiple_of(g * brows, brows), brows), :]
+        for i in range(ga - 1):
+            m_copy(b, i).wait_recv()
+            total = total + mrows[b, i]
+        erow[b] = total
+
+        @pl.when(odd == 1)
+        def _():
+            if b == 0:
+                s_copy.wait_recv()
+            erow[b] = total + taken_in[:, b]
+
+        total = erow[b]
+        first = b * BANDS + g * brows
+        row_at = lax.broadcasted_iota(jnp.int32, (brows, nb), 0) + first
+        col_at = lax.broadcasted_iota(jnp.int32, (brows, nb), 1)
+        erow[b, 0] = jnp.where(row_at == col_at, 1.0, 0.0) - total[0]
+        erow[b, 1] = -total[1]
+        for i in range(ga - 1):
+            e_copy(b, i).start()
+        efull[:, pl.ds(pl.multiple_of(first, brows), brows), :] = erow[b]
+
+    phase("project0")
+    lax.fori_loop(0, 4, project, 0)
+
     intersect(0)
     phase("project1")
     lax.fori_loop(4, 6, project, 0)
     intersect(1)
-    settle(0)
+    phase("take")
+
+    @pl.when(even)
+    def _():
+        take()
+
     phase("project2")
     lax.fori_loop(6, ga, project, 0)
+    nb_turn(2)
     intersect(2)
+    intersect(3)
+    phase("give_back")
+
+    @pl.when(even)
+    def _():
+        give_back()
+
+    settle(0)
+    nb_turn(3)
     settle(1)
-    intersect(3)
     settle(2)
     settle(3)
-
-    phase("token")
-
-    @pl.when(odd == 1)
-    def _():
-        pl.semaphore_signal(ready_sem, inc=1, device_id={"ka": mate, "ga": g}, device_id_type=MESH)
-
-    @pl.when(odd == 0)
-    def _():
-        pl.semaphore_wait(ready_sem, 1)
-
-    for i in range(EARLY, ga - 1):
-        for copy in piece_copies(i):
-            copy.start()
+    phase("take_last")
+
+    @pl.when(k == 0)
+    def _():
+        take()
+        give_back()
 
     phase("e_ag")
     for b in range(blocks):
         for i in range(ga - 1):
             e_copy(b, i).wait_recv()
+
+    pl.semaphore_signal(ready_sem, inc=1, device_id={"ka": mate, "ga": g}, device_id_type=MESH)
 
     phase("newton")
     e_re, e_im = efull[0], efull[1]
@@ -255,6 +369,7 @@
     mine = pl.ds(pl.multiple_of(g * rows, rows), rows)
     x_copy = remote(xfull, xmate, x_send, x_recv, mate, g)
     onward = remote(trow.at[1], tin, t_send, t_recv, ka_at(2), g)
+    first = remote(xfull.at[:, mine, :], tin, t_send, t_recv, 1, g)
 
     def same_copy(i):
         return remote(trow.at[1], tfull.at[:, mine, :], g_send.at[i], g_recv.at[i], k, ga_at(i))
@@ -262,15 +377,54 @@
     def mate_copy(i):
         return remote(trow.at[0], tfull.at[:, mine, :], h_send.at[i], g_recv.at[i], mate, ga_at(i))
 
-    @pl.when(odd == 0)
+    @pl.when(k == 0)
+    def _():
+        first.start()
+
+    @pl.when(jnp.logical_and(odd == 0, k > 0))
     def _():
         x_copy.start()
 
+    phase("token")
+    pl.semaphore_wait(ready_sem, 1)
+    for i in range(EARLY, ga - 2):
+        for copy in piece_copies(i):
+            copy.start()
+
+    z_copies = (
+        remote(z_piece, z_in, z_send.at[0], z_recv.at[0], k, ring_at * 2 + 1 - place),
+        remote(z_scale, z_in_scale, z_send.at[1], z_recv.at[1], k, ring_at * 2 + 1 - place),
+    )
+
+    def sum_ring():
+        phase("p_wait")
+        for i in range(ga - 2):
+            for copy in piece_copies(i):
+                copy.wait_recv()
+        phase("p_sum")
+        out = part[ga - 2]
+        for i in (0, 1, 4):
+            out = out + decoded(in_pieces[i], in_scales[i])
+        code, scale = coded(out)
+        z_piece[...] = code
+        z_scale[...] = scale
+        for copy in z_copies:
+            copy.start()
+        out = part[ga - 1]
+        for i in (2, 3, 5):
+            out = out + decoded(in_pieces[i], in_scales[i])
+        part[ga - 1] = out
+
+    late = jnp.logical_or(odd == 0, k > LATE)
+
+    @pl.when(late)
+    def _():
+        sum_ring()
+
+    phase("chain")
+
     @pl.when(odd == 1)
     def _():
-        phase("x_wait")
-        x_copy.wait_recv()
-
         def keep(re, im):
             high, low = split(re)
             qhigh[:, 0:nb] = high
@@ -288,14 +442,14 @@
         @pl.when(k == 1)
         def _():
             keep(xfull[0], xfull[1])
-            tin[...] = xmate[:, mine, :]
 
         @pl.when(k > 1)
         def _():
+            x_copy.wait_recv()
             keep(*cmul(xmate[...].reshape(2 * nb, nb), xfull[0], xfull[1]))
-            phase("t_in")
-            onward.wait_recv()
-
+
+        phase("t_in")
+        onward.wait_recv()
         phase("t_step")
         left = tin[...].reshape(2 * rows, nb)
         re, im = step(left, qhigh[...], qlow[...])
@@ -325,14 +479,15 @@
         for i in range(ga):
             mate_copy(i).start()
 
-    phase("p_wait")
-    for i in range(ga - 1):
-        for copy in piece_copies(i):
-            copy.wait_recv()
-    phase("p_sum")
-    whole = part[...]
-    for i in range(ga - 1):
-        whole = whole + in_pieces[i].astype(jnp.int32).astype(F32) * in_scales[i, 0:1, :]
+    @pl.when(jnp.logical_not(late))
+    def _():
+        sum_ring()
+
+    phase("z_wait")
+    for copy in z_copies:
+        copy.wait_recv()
+    phase("z_sum")
+    whole = part[ga - 1] + decoded(z_in[...], z_in_scale[...])
     b_both = jnp.concatenate([whole[0:nb, 0:cols].T, whole[nb:2 * nb, 0:cols].T], axis=0)
     d_re = whole[0:nb, cols:2 * cols].T
     d_im = whole[nb:2 * nb, cols:2 * cols].T
@@ -376,23 +531,45 @@
 
     phase("drain")
     for b in range(blocks):
-        nb_copy(b).wait_send()
+        for r in range(2):
+            nb_copy(b, r).wait_send()
+
+        @pl.when(odd == 1)
+        def _():
+            for r in range(2, 4):
+                nb_copy(b, r).wait_send()
+
         for i in range(ga - 1):
             m_copy(b, i).wait_send()
             e_copy(b, i).wait_send()
-    for i in range(ga - 1):
+    for i in range(ga - 2):
         for copy in piece_copies(i):
             copy.wait_send()
+    for copy in z_copies:
+        copy.wait_send()
+    for i in range(ga - 1):
         along_ga(i).wait_send()
     for i in range(ka - 1):
         along_ka(i).wait_send()
 
     @pl.when(odd == 0)
     def _():
+        for i in range(ga - 1):
+            a_copy(i).wait_send()
+        s_copy.wait_send()
+
+    @pl.when(k == 0)
+    def _():
+        first.wait_send()
+
+    @pl.when(jnp.logical_and(odd == 0, k > 0))
+    def _():
         x_copy.wait_send()
 
     @pl.when(odd == 1)
     def _():
+        for r in range(2):
+            c_copy(r).wait_send()
         for i in range(1, ga):
             same_copy(i).wait_send()
         for i in range(ga):
@@ -426,12 +603,21 @@
             pltpu.VMEM((2 * half, nb), BF16),
             pltpu.VMEM((2 * nb, 2 * half), BF16),
             pltpu.VMEM((blocks, BANDS, 2 * half), BF16),
+            pltpu.VMEM((2, SHARED, nb), BF16),
+            pltpu.VMEM((2, blocks, BANDS, nb), F32),
+            pltpu.VMEM((ga - 1, 2, blocks, brows, nb), F32),
+            pltpu.VMEM((2, blocks, brows, nb), F32),
+            pltpu.VMEM((2, blocks, brows, nb), F32),
             pltpu.VMEM((3, 2, half, 2 * cols), BF16),
-            pltpu.VMEM((2 * nb, 2 * cols), F32),
-            pltpu.VMEM((ga - 1, 2 * nb, 2 * cols), I16),
-            pltpu.VMEM((ga - 1, 8, 2 * cols), F32),
-            pltpu.VMEM((ga - 1, 2 * nb, 2 * cols), I16),
-            pltpu.VMEM((ga - 1, 8, 2 * cols), F32),
+            pltpu.VMEM((ga, 2 * nb, 2 * cols), F32),
+            pltpu.VMEM((ga - 2, 2 * nb, 2 * cols), I16),
+            pltpu.VMEM((ga - 2, 8, 2 * cols), F32),
+            pltpu.VMEM((ga - 2, 2 * nb, 2 * cols), I16),
+            pltpu.VMEM((ga - 2, 8, 2 * cols), F32),
+            pltpu.VMEM((2 * nb, 2 * cols), I16),
+            pltpu.VMEM((8, 2 * cols), F32),
+            pltpu.VMEM((2 * nb, 2 * cols), I16),
+            pltpu.VMEM((8, 2 * cols), F32),
             pltpu.VMEM((blocks, 2, BANDS, nb), F32),
             pltpu.VMEM((blocks, ga - 1, 2, brows, nb), F32),
             pltpu.VMEM((blocks, 2, brows, nb), F32),
@@ -445,7 +631,9 @@
             pltpu.VMEM((2, nb, nb), F32),
             pltpu.VMEM((ka, 8, 128), F32),
             pltpu.VMEM((ga, 8, 128), F32),
-            dma, dma((3, 2)), dma((blocks,)), dma((blocks,)), dma((ga - 1, 2)), dma((ga - 1, 2)),
+            dma, dma((3, 2)), dma((blocks, 4)), dma((blocks, 4)), dma((2,)), dma((2,)),
+            dma((2,)), dma((2,)), dma((ga - 1,)), dma((ga - 1,)), dma, dma,
+            dma((ga - 2, 2)), dma((ga - 2, 2)),
             dma((blocks, ga - 1)), dma((blocks, ga - 1)), dma((blocks, ga - 1)), dma((blocks, ga - 1)),
             dma, dma, dma, dma, dma((ga,)), dma((ga,)), dma((ga,)),
             dma((ka - 1,)), dma((ka - 1,)), dma((ga - 1,)), dma((ga - 1,)), dma,
@@ -456,7 +644,7 @@
         name="string",
     )(
         coeffs.reshape(2 * half, nb), projectors, proj_deriv,
-        shift_map.reshape(1, half), atom_of.reshape(ga, cols),
+        shift_map.reshape(half // 128, 128), atom_of.reshape(ga, cols),
     )
     return transport[None], forces.reshape(128)
 

time: 111 us -> 100 us (0.901)
  Pallas kernels: 106 us -> 96.2 us
  local copies, waits for them, and re-layouts: 4.27 us -> 2.97 us
    pallas_call x1, Pallas kernels: 106 us -> 96.2 us  [local(): pl.pallas_call(functools.partial(kernel, ka, ga), out_shape=(jax.ShapeDty...]
    reshape x1 -> x0, local copies, waits for them, and re-layouts: 1.3 us -> none  [local(): shift_map.reshape(1, half)]
where the time goes in v3:
time: 100 us; the launch traced here: 99.8 us
  Pallas kernels  96.2 us (96%)
  local copies, waits for them, and re-layouts  2.97 us (3%)
    pallas_call x1, Pallas kernels, local(): pl.pallas_call(functools.partial(kernel, ka, ga), out_shape=(jax.ShapeDty...  96.2 us
    unnamed x2, local copies, waits for them, and re-layouts  2.97 us

profile of v3, /device:TPU:0, one launch (start us, length us, event | category | flops | bytes accessed | tf_op | source)
XLA Modules:
  0.0 99.8 jit_solution(12169751861673561157)
XLA Ops:
  0.6 96.2 %string.1 = (f32[2,256,256]{2,1,0:T(8,128)}, f32[1,128]{1,0:T(1,128)}) custom-call(bf16[3840,256]{1,0:T(8,128)(2,1)} %bitcast.5, bf16[2,1920,1024]{2,1,0:T(8,128)(2,1)} %proj.1, bf16[2,1920,1024]{2,1,0:T(8,128)(2,1)} %deriv.1, s32[15,128]{1,0:T(8,128)} %bitcast.7, s32[8,128]{1,0:T(8,128)} %bitcast.8), custom_call_target="tpu_custom_call" | custom-call | tf_op jit(solution)/shard_map/string/pallas_call | solution.py:596
  96.9 1.9 %copy.9 = f32[1,2,256,256]{3,2,1,0:T(8,128)} copy(f32[1,2,256,256]{3,2,1,0:T(8,128)} %bitcast.6) | data formatting | bytes 1048576
  98.7 1.1 %copy.10 = f32[128]{0:T(128)} copy(f32[128]{0:T(128)} %bitcast.9) | data formatting | bytes 1024

commit v4 on v3

--- a/solution.py
+++ b/solution.py
@@ -14,7 +14,9 @@
 BANDS = 64
 SHARED = 640
 EARLY = 2
-LATE = 8
+MIDDLE = 4
+HURRY = 12
+LATE = 10
 
 
 def split(value):
@@ -44,7 +46,7 @@
 def kernel(
     ka, ga, coeffs, proj, deriv, shift, atoms, transport, forces,
     own, moved, lhs, nbt, cnat, taken, taken_rows, taken_sum, taken_in, rhs, part, pieces, scales, in_pieces, in_scales, z_piece, z_scale, z_in, z_in_scale, mpart, mrows, erow, efull,
-    xfull, xmate, qhigh, qlow, tin, trow, tfull, fka, fga,
+    xfull, xmate, qhigh, qlow, tin, trow, tcode, tscale, tcodes, tscales, tfull, fka, fga,
     load_sem, rhs_sem, nb_send, nb_recv, z_send, z_recv, c_send, c_recv, a_send, a_recv, s_send, s_recv, p_send, p_recv, m_send, m_recv, e_send, e_recv,
     x_send, x_recv, t_send, t_recv, g_send, g_recv, h_send, f_send, f_recv, l_send, l_recv, out_sem, ready_sem,
 ):
@@ -200,10 +202,17 @@
     def coded(values):
         top = jnp.maximum(jnp.max(jnp.abs(values), axis=0, keepdims=True), 1e-30)
         code = jnp.round(values * (32767.0 / top)).astype(jnp.int32).astype(I16)
-        return code, jnp.broadcast_to(top * (1.0 / 32767.0), (8, 2 * cols))
+        return code, jnp.broadcast_to(top * (1.0 / 32767.0), (8, values.shape[1]))
 
     def decoded(code, scale):
         return code.astype(jnp.int32).astype(F32) * scale[0:1, :]
+
+    hurry = k < HURRY
+
+    def send(first, last):
+        for i in range(first, last):
+            for copy in piece_copies(i):
+                copy.start()
 
     def project(i, carry):
         for copy in rhs_loads(i):
@@ -325,19 +334,24 @@
     def _():
         take()
 
+    send(EARLY, MIDDLE)
     phase("project2")
     lax.fori_loop(6, ga, project, 0)
-    nb_turn(2)
     intersect(2)
     intersect(3)
+    nb_turn(2)
+    nb_turn(3)
     phase("give_back")
 
     @pl.when(even)
     def _():
         give_back()
 
+    @pl.when(jnp.logical_not(hurry))
+    def _():
+        send(MIDDLE, ga - 2)
+
     settle(0)
-    nb_turn(3)
     settle(1)
     settle(2)
     settle(3)
@@ -346,14 +360,15 @@
     @pl.when(k == 0)
     def _():
         take()
-        give_back()
 
     phase("e_ag")
     for b in range(blocks):
         for i in range(ga - 1):
             e_copy(b, i).wait_recv()
 
-    pl.semaphore_signal(ready_sem, inc=1, device_id={"ka": mate, "ga": g}, device_id_type=MESH)
+    @pl.when(hurry)
+    def _():
+        pl.semaphore_signal(ready_sem, inc=1, device_id={"ka": mate, "ga": g}, device_id_type=MESH)
 
     phase("newton")
     e_re, e_im = efull[0], efull[1]
@@ -372,24 +387,36 @@
     first = remote(xfull.at[:, mine, :], tin, t_send, t_recv, 1, g)
 
     def same_copy(i):
-        return remote(trow.at[1], tfull.at[:, mine, :], g_send.at[i], g_recv.at[i], k, ga_at(i))
+        return (
+            remote(tcode.at[1], tcodes.at[g], g_send.at[i, 0], g_recv.at[i, 0], k, ga_at(i)),
+            remote(tscale.at[1], tscales.at[g], g_send.at[i, 1], g_recv.at[i, 1], k, ga_at(i)),
+        )
 
     def mate_copy(i):
-        return remote(trow.at[0], tfull.at[:, mine, :], h_send.at[i], g_recv.at[i], mate, ga_at(i))
+        return (
+            remote(tcode.at[0], tcodes.at[g], h_send.at[i, 0], g_recv.at[i, 0], mate, ga_at(i)),
+            remote(tscale.at[0], tscales.at[g], h_send.at[i, 1], g_recv.at[i, 1], mate, ga_at(i)),
+        )
+
+    def encode(which):
+        code, scale = coded(trow[which].reshape(2 * rows, nb))
+        tcode[which] = code
+        tscale[which] = scale
 
     @pl.when(k == 0)
     def _():
         first.start()
+        give_back()
 
     @pl.when(jnp.logical_and(odd == 0, k > 0))
     def _():
         x_copy.start()
 
     phase("token")
-    pl.semaphore_wait(ready_sem, 1)
-    for i in range(EARLY, ga - 2):
-        for copy in piece_copies(i):
-            copy.start()
+    @pl.when(hurry)
+    def _():
+        pl.semaphore_wait(ready_sem, 1)
+        send(MIDDLE, ga - 2)
 
     z_copies = (
         remote(z_piece, z_in, z_send.at[0], z_recv.at[0], k, ring_at * 2 + 1 - place),
@@ -460,9 +487,12 @@
         def _():
             onward.start()
 
+        encode(1)
         for i in range(1, ga):
-            same_copy(i).start()
-        tfull[:, mine, :] = trow[1]
+            for copy in same_copy(i):
+                copy.start()
+        tcodes[g] = tcode[1]
+        tscales[g] = tscale[1]
 
         phase("t_mate")
 
@@ -476,8 +506,10 @@
             trow[0, 0] = re
             trow[0, 1] = im
 
+        encode(0)
         for i in range(ga):
-            mate_copy(i).start()
+            for copy in mate_copy(i):
+                copy.start()
 
     @pl.when(jnp.logical_not(late))
     def _():
@@ -495,11 +527,16 @@
 
     phase("t_ag")
     for i in range(1, ga):
-        same_copy(i).wait_recv()
+        for copy in same_copy(i):
+            copy.wait_recv()
 
     @pl.when(odd == 0)
     def _():
-        mate_copy(0).wait_recv()
+        for copy in mate_copy(0):
+            copy.wait_recv()
+
+    for i in range(ga):
+        tfull[:, i * rows:(i + 1) * rows, :] = decoded(tcodes[i], tscales[i]).reshape(2, rows, nb)
 
     phase("w")
     out_copy = pltpu.make_async_copy(tfull, transport, out_sem)
@@ -508,7 +545,7 @@
     per_proj = jnp.sum(d_re * w_im - d_im * w_re, axis=1, keepdims=True) * (1.0 / ka)
     atom_ids = lax.broadcasted_iota(jnp.int32, (cols, 128), 1).astype(F32)
     force = jnp.sum(jnp.where(atom_column == atom_ids, per_proj, 0.0), axis=0, keepdims=True)
-    fka[k] = jnp.broadcast_to(force, (8, 128))
+    fka[k] = force
 
     def along_ka(i):
         return remote(fka.at[k], fka.at[k], f_send.at[i], f_recv.at[i], ka_at(1 + i), g)
@@ -527,7 +564,7 @@
         along_ga(i).start()
     for i in range(ga - 1):
         along_ga(i).wait_recv()
-    forces[...] = jnp.sum(fga[...], axis=0)[0:1]
+    forces[...] = jnp.sum(fga[...], axis=0)
 
     phase("drain")
     for b in range(blocks):
@@ -571,9 +608,11 @@
         for r in range(2):
             c_copy(r).wait_send()
         for i in range(1, ga):
-            same_copy(i).wait_send()
+            for copy in same_copy(i):
+                copy.wait_send()
         for i in range(ga):
-            mate_copy(i).wait_send()
+            for copy in mate_copy(i):
+                copy.wait_send()
 
         @pl.when(k < ka - 1)
         def _():
@@ -628,14 +667,18 @@
             pltpu.VMEM((nb, 2 * nb), BF16),
             pltpu.VMEM((2, rows, nb), F32),
             pltpu.VMEM((2, 2, rows, nb), F32),
+            pltpu.VMEM((2, 2 * rows, nb), I16),
+            pltpu.VMEM((2, 8, nb), F32),
+            pltpu.VMEM((ga, 2 * rows, nb), I16),
+            pltpu.VMEM((ga, 8, nb), F32),
             pltpu.VMEM((2, nb, nb), F32),
-            pltpu.VMEM((ka, 8, 128), F32),
-            pltpu.VMEM((ga, 8, 128), F32),
+            pltpu.VMEM((ka, 1, 128), F32),
+            pltpu.VMEM((ga, 1, 128), F32),
             dma, dma((3, 2)), dma((blocks, 4)), dma((blocks, 4)), dma((2,)), dma((2,)),
             dma((2,)), dma((2,)), dma((ga - 1,)), dma((ga - 1,)), dma, dma,
             dma((ga - 2, 2)), dma((ga - 2, 2)),
             dma((blocks, ga - 1)), dma((blocks, ga - 1)), dma((blocks, ga - 1)), dma((blocks, ga - 1)),
-            dma, dma, dma, dma, dma((ga,)), dma((ga,)), dma((ga,)),
+            dma, dma, dma, dma, dma((ga, 2)), dma((ga, 2)), dma((ga, 2)),
             dma((ka - 1,)), dma((ka - 1,)), dma((ga - 1,)), dma((ga - 1,)), dma,
             pltpu.SemaphoreType.REGULAR,
         ],

time: 100 us -> 88.3 us (0.88)
  Pallas kernels: 96.2 us -> 84.5 us
    pallas_call x1, Pallas kernels: 96.2 us -> 84.5 us  [local(): pl.pallas_call(functools.partial(kernel, ka, ga), out_shape=(jax.ShapeDty...]
where the time goes in v4:
time: 88.3 us; the launch traced here: 88.1 us
  Pallas kernels  84.5 us (96%)
  local copies, waits for them, and re-layouts  2.97 us (3%)
    pallas_call x1, Pallas kernels, local(): pl.pallas_call(functools.partial(kernel, ka, ga), out_shape=(jax.ShapeDty...  84.5 us
    unnamed x2, local copies, waits for them, and re-layouts  2.97 us

profile of v4, /device:TPU:0, one launch (start us, length us, event | category | flops | bytes accessed | tf_op | source)
XLA Modules:
  0.0 88.1 jit_solution(6801707684696370604)
XLA Ops:
  0.6 84.5 %string.1 = (f32[2,256,256]{2,1,0:T(8,128)}, f32[1,128]{1,0:T(1,128)}) custom-call(bf16[3840,256]{1,0:T(8,128)(2,1)} %bitcast.5, bf16[2,1920,1024]{2,1,0:T(8,128)(2,1)} %proj.1, bf16[2,1920,1024]{2,1,0:T(8,128)(2,1)} %deriv.1, s32[15,128]{1,0:T(8,128)} %bitcast.7, s32[8,128]{1,0:T(8,128)} %bitcast.8), custom_call_target="tpu_custom_call" | custom-call | tf_op jit(solution)/shard_map/string/pallas_call | solution.py:635
  85.1 1.9 %copy.9 = f32[1,2,256,256]{3,2,1,0:T(8,128)} copy(f32[1,2,256,256]{3,2,1,0:T(8,128)} %bitcast.6) | data formatting | bytes 1048576
  87.0 1.1 %copy.10 = f32[128]{0:T(128)} copy(f32[128]{0:T(128)} %bitcast.9) | data formatting | bytes 1024

commit v5 on v4

--- a/solution.py
+++ b/solution.py
@@ -13,8 +13,9 @@
 I16 = jnp.int16
 BANDS = 64
 SHARED = 640
+TURNED = 1024
 EARLY = 2
-MIDDLE = 4
+FIRST = 4
 HURRY = 12
 LATE = 10
 
@@ -45,7 +46,7 @@
 
 def kernel(
     ka, ga, coeffs, proj, deriv, shift, atoms, transport, forces,
-    own, moved, lhs, nbt, cnat, taken, taken_rows, taken_sum, taken_in, rhs, part, pieces, scales, in_pieces, in_scales, z_piece, z_scale, z_in, z_in_scale, mpart, mrows, erow, efull,
+    own, moved, lhs, nbt, cnat, taken, taken_rows, taken_sum, taken_in, rhs, part, pieces, scales, in_pieces, in_scales, z_piece, z_scale, z_in, z_in_scale, mpart, mrows, erow, ecode, escale, ecodes, escales, efull,
     xfull, xmate, qhigh, qlow, tin, trow, tcode, tscale, tcodes, tscales, tfull, fka, fga,
     load_sem, rhs_sem, nb_send, nb_recv, z_send, z_recv, c_send, c_recv, a_send, a_recv, s_send, s_recv, p_send, p_recv, m_send, m_recv, e_send, e_recv,
     x_send, x_recv, t_send, t_recv, g_send, g_recv, h_send, f_send, f_recv, l_send, l_recv, out_sem, ready_sem,
@@ -67,6 +68,7 @@
     blocks = nb // BANDS
     brows = BANDS // ga
     kept = half - SHARED
+    least = half - TURNED
     k = lax.axis_index("ka")
     g = lax.axis_index("ga")
     odd = lax.rem(k, 2)
@@ -135,38 +137,35 @@
         lhs[nb:2 * nb, at:at + width] = im
         lhs[nb:2 * nb, half + at:half + at + width] = -re
 
-    ranges = ((0, kept), (half, kept), (kept, SHARED), (half + kept, SHARED))
+    plane = ka // 2
+    turn_back = lax.rem(k, plane) == 0
+    turn_on = lax.rem(k, plane) == plane - 1
+    ranges = tuple(
+        (part_at + first, last - first) for first, last in ((0, least), (least, kept), (kept, half)) for part_at in (0, half))
 
     def nb_copy(b, r):
         at = pl.ds(*ranges[r])
         return remote(lhs.at[pl.ds(b * BANDS, BANDS), at], nbt.at[b, :, at], nb_send.at[b, r], nb_recv.at[b, r],
                       ka_at(ka - 1), g)
 
-    plane = ka // 2
-    turn = lax.rem(k, plane) == 0
-
-    def nb_start(b):
-        for r in range(2):
-            nb_copy(b, r).start()
-
-    def nb_turn(b):
-        @pl.when(turn)
-        def _():
-            nb_start(b)
-
-    nb_start(0)
-    nb_start(1)
-
-    @pl.when(jnp.logical_not(turn))
-    def _():
-        nb_start(2)
-        nb_start(3)
-
-    @pl.when(odd == 1)
-    def _():
-        for b in range(blocks):
-            for r in range(2, 4):
-                nb_copy(b, r).start()
+    def nb_each(act, b, sent):
+        short = turn_back if sent else turn_on
+        whole = odd == 1 if sent else odd == 0
+        for r in (0, 1):
+            act(nb_copy(b, r))
+
+        @pl.when(jnp.logical_not(short))
+        def _():
+            for r in (2, 3):
+                act(nb_copy(b, r))
+
+        @pl.when(whole)
+        def _():
+            for r in (4, 5):
+                act(nb_copy(b, r))
+
+    for b in range(blocks):
+        nb_each(lambda copy: copy.start(), b, True)
 
     phase("permute")
 
@@ -186,28 +185,50 @@
         own[...] = moved[...]
 
     def c_copy(r):
-        return remote(own.at[pl.ds(kept + r * half, SHARED)], cnat.at[r], c_send.at[r], c_recv.at[r], ka_at(1), g)
+        first, count = ranges[2 + r]
+        part_at = half * (r % 2)
+        return remote(own.at[pl.ds(first, count)], cnat.at[r % 2, pl.ds(first - part_at - least, count)],
+                      c_send.at[r], c_recv.at[r], ka_at(1), g)
+
+    def c_each(act, short):
+        for r in (2, 3):
+            act(c_copy(r))
+
+        @pl.when(short)
+        def _():
+            for r in (0, 1):
+                act(c_copy(r))
 
     @pl.when(odd == 1)
     def _():
-        for r in range(2):
-            c_copy(r).start()
+        c_each(lambda copy: copy.start(), turn_on)
+
+    def piece_to(i):
+        across = (i // 4) * (1 - lax.rem(i, 2))
+        return along_ring((1 - across) * block_of(i)[0]) + place + across * (1 - 2 * place)
 
     def piece_copies(i):
         return (
-            remote(pieces.at[i], in_pieces.at[i], p_send.at[i, 0], p_recv.at[i, 0], k, along_ring(block_of(i)[0]) + place),
-            remote(scales.at[i], in_scales.at[i], p_send.at[i, 1], p_recv.at[i, 1], k, along_ring(block_of(i)[0]) + place),
+            remote(pieces.at[i], in_pieces.at[i], p_send.at[i, 0], p_recv.at[i, 0], k, piece_to(i)),
+            remote(scales.at[i], in_scales.at[i], p_send.at[i, 1], p_recv.at[i, 1], k, piece_to(i)),
         )
 
     def coded(values):
         top = jnp.maximum(jnp.max(jnp.abs(values), axis=0, keepdims=True), 1e-30)
         code = jnp.round(values * (32767.0 / top)).astype(jnp.int32).astype(I16)
-        return code, jnp.broadcast_to(top * (1.0 / 32767.0), (8, values.shape[1]))
+        return code, top * (1.0 / 32767.0)
 
     def decoded(code, scale):
-        return code.astype(jnp.int32).astype(F32) * scale[0:1, :]
+        return code.astype(jnp.int32).astype(F32) * scale
 
     hurry = k < HURRY
+
+    def combine():
+        for copy in piece_copies(4):
+            copy.wait_recv()
+        code, scale = coded(part[5] + decoded(in_pieces[4], in_scales[4]))
+        pieces[5] = code
+        scales[5] = scale
 
     def send(first, last):
         for i in range(first, last):
@@ -225,7 +246,7 @@
 
         part[i] = dot(lhs[...], rhs[lax.rem(i, 3)].reshape(2 * half, 2 * cols))
 
-        @pl.when(i < ga - 2)
+        @pl.when(i < ga - 3)
         def _():
             code, scale = coded(part[i])
             pieces[i] = code
@@ -252,17 +273,18 @@
             by_im = dot(jnp.concatenate([im, -re], axis=0), own[half:half + count, :])
             mpart[b] = (by_re + by_im).reshape(2, BANDS, nb)
 
-        for r in range(2):
-            nb_copy(b, r).wait_recv()
-
-        @pl.when(odd == 1)
+        nb_each(lambda copy: copy.wait_recv(), b, False)
+
+        @pl.when(turn_on)
+        def _():
+            over(least)
+
+        @pl.when(jnp.logical_and(odd == 1, jnp.logical_not(turn_on)))
         def _():
             over(kept)
 
         @pl.when(odd == 0)
         def _():
-            for r in range(2, 4):
-                nb_copy(b, r).wait_recv()
             over(half)
 
         phase(f"m_dot{b}")
@@ -276,10 +298,21 @@
     s_copy = remote(taken_sum, taken_in, s_send, s_recv, ka_at(ka - 1), g)
 
     def take():
-        for r in range(2):
-            c_copy(r).wait_recv()
-        out = dot(lhs[:, kept:half], cnat[0]) + dot(lhs[:, half + kept:2 * half], cnat[1])
-        taken[...] = out.reshape(2, blocks, BANDS, nb)
+        c_each(lambda copy: copy.wait_recv(), turn_back)
+
+        def from_wave(first):
+            out = dot(lhs[:, first:half], cnat[0, first - least:])
+            out = out + dot(lhs[:, half + first:2 * half], cnat[1, first - least:])
+            taken[...] = out.reshape(2, blocks, BANDS, nb)
+
+        @pl.when(turn_back)
+        def _():
+            from_wave(least)
+
+        @pl.when(jnp.logical_not(turn_back))
+        def _():
+            from_wave(kept)
+
         for i in range(ga - 1):
             a_copy(i).start()
 
@@ -293,9 +326,28 @@
 
     even = jnp.logical_and(odd == 0, k > 0)
 
-    def e_copy(b, i):
-        at = pl.ds(pl.multiple_of(b * BANDS + g * brows, brows), brows)
-        return remote(erow.at[b], efull.at[:, at, :], e_send.at[b, i], e_recv.at[b, i], k, ga_at(1 + i))
+    spans = ((0, blocks - 1), (blocks - 1, blocks))
+
+    def span_rows(span):
+        return pl.ds(2 * brows * spans[span][0], 2 * brows * (spans[span][1] - spans[span][0]))
+
+    def e_copies(span, i):
+        to = ga_at(1 + i)
+        return (
+            remote(ecode.at[span_rows(span)], ecodes.at[g, span_rows(span)], e_send.at[span, i, 0], e_recv.at[span, i, 0], k, to),
+            remote(escale.at[span], escales.at[span, g], e_send.at[span, i, 1], e_recv.at[span, i, 1], k, to),
+        )
+
+    def spread(span):
+        first, last = spans[span]
+        code, scale = coded(erow[first:last].reshape(2 * brows * (last - first), nb))
+        ecode[span_rows(span), :] = code
+        escale[span] = scale
+        for i in range(ga - 1):
+            for copy in e_copies(span, i):
+                copy.start()
+        ecodes[g, span_rows(span), :] = code
+        escales[span, g] = scale
 
     def settle(b):
         phase(f"m_rs{b}")
@@ -317,9 +369,6 @@
         col_at = lax.broadcasted_iota(jnp.int32, (brows, nb), 1)
         erow[b, 0] = jnp.where(row_at == col_at, 1.0, 0.0) - total[0]
         erow[b, 1] = -total[1]
-        for i in range(ga - 1):
-            e_copy(b, i).start()
-        efull[:, pl.ds(pl.multiple_of(first, brows), brows), :] = erow[b]
 
     phase("project0")
     lax.fori_loop(0, 4, project, 0)
@@ -334,27 +383,41 @@
     def _():
         take()
 
-    send(EARLY, MIDDLE)
+
+    @pl.when(k >= FIRST)
+    def _():
+        send(EARLY, 4)
+
     phase("project2")
     lax.fori_loop(6, ga, project, 0)
     intersect(2)
     intersect(3)
-    nb_turn(2)
-    nb_turn(3)
     phase("give_back")
 
     @pl.when(even)
     def _():
         give_back()
 
-    @pl.when(jnp.logical_not(hurry))
-    def _():
-        send(MIDDLE, ga - 2)
+    @pl.when(k >= FIRST)
+    def _():
+        send(4, 5)
 
     settle(0)
     settle(1)
     settle(2)
+    spread(0)
     settle(3)
+    spread(1)
+    phase("combine")
+
+    @pl.when(k >= FIRST)
+    def _():
+        combine()
+
+    @pl.when(jnp.logical_not(hurry))
+    def _():
+        send(5, 6)
+
     phase("take_last")
 
     @pl.when(k == 0)
@@ -362,9 +425,16 @@
         take()
 
     phase("e_ag")
-    for b in range(blocks):
-        for i in range(ga - 1):
-            e_copy(b, i).wait_recv()
+    for span in range(2):
+        for i in range(ga - 1):
+            for copy in e_copies(span, i):
+                copy.wait_recv()
+    for i in range(ga):
+        for b in range(blocks):
+            span = b // (blocks - 1)
+            code = ecodes[i, 2 * brows * b:2 * brows * (b + 1), :]
+            efull[:, b * BANDS + i * brows:b * BANDS + (i + 1) * brows, :] = decoded(code, escales[span, i]).reshape(
+                2, brows, nb)
 
     @pl.when(hurry)
     def _():
@@ -383,8 +453,14 @@
     phase("chain")
     mine = pl.ds(pl.multiple_of(g * rows, rows), rows)
     x_copy = remote(xfull, xmate, x_send, x_recv, mate, g)
-    onward = remote(trow.at[1], tin, t_send, t_recv, ka_at(2), g)
-    first = remote(xfull.at[:, mine, :], tin, t_send, t_recv, 1, g)
+    few = rows // 2
+
+    def onward(h):
+        return remote(trow.at[1, h], tin.at[h], t_send.at[h], t_recv.at[h], ka_at(2), g)
+
+    def first(h):
+        at = pl.ds(pl.multiple_of(g * rows + h * few, few), few)
+        return remote(xfull.at[:, at, :], tin.at[h], t_send.at[h], t_recv.at[h], 1, g)
 
     def same_copy(i):
         return (
@@ -405,7 +481,8 @@
 
     @pl.when(k == 0)
     def _():
-        first.start()
+        first(0).start()
+        first(1).start()
         give_back()
 
     @pl.when(jnp.logical_and(odd == 0, k > 0))
@@ -416,7 +493,14 @@
     @pl.when(hurry)
     def _():
         pl.semaphore_wait(ready_sem, 1)
-        send(MIDDLE, ga - 2)
+
+        @pl.when(k < FIRST)
+        def _():
+            send(EARLY, 5)
+
+        @pl.when(k >= FIRST)
+        def _():
+            send(5, 6)
 
     z_copies = (
         remote(z_piece, z_in, z_send.at[0], z_recv.at[0], k, ring_at * 2 + 1 - place),
@@ -424,13 +508,20 @@
     )
 
     def sum_ring():
+        phase("p_combine")
+
+        @pl.when(k < FIRST)
+        def _():
+            combine()
+            send(5, 6)
+
         phase("p_wait")
-        for i in range(ga - 2):
+        for i in (0, 1, 2, 3, 5):
             for copy in piece_copies(i):
                 copy.wait_recv()
         phase("p_sum")
         out = part[ga - 2]
-        for i in (0, 1, 4):
+        for i in (0, 1):
             out = out + decoded(in_pieces[i], in_scales[i])
         code, scale = coded(out)
         z_piece[...] = code
@@ -475,17 +566,17 @@
             x_copy.wait_recv()
             keep(*cmul(xmate[...].reshape(2 * nb, nb), xfull[0], xfull[1]))
 
-        phase("t_in")
-        onward.wait_recv()
-        phase("t_step")
-        left = tin[...].reshape(2 * rows, nb)
-        re, im = step(left, qhigh[...], qlow[...])
-        trow[1, 0] = re
-        trow[1, 1] = im
-
-        @pl.when(k < ka - 1)
-        def _():
-            onward.start()
+        for h in range(2):
+            phase("t_in")
+            onward(h).wait_recv()
+            phase("t_step")
+            re, im = step(tin[h].reshape(rows, nb), qhigh[...], qlow[...])
+            trow[1, h, 0] = re
+            trow[1, h, 1] = im
+
+            @pl.when(k < ka - 1)
+            def _():
+                onward(h).start()
 
         encode(1)
         for i in range(1, ga):
@@ -502,9 +593,11 @@
 
         @pl.when(k > 1)
         def _():
+            left = jnp.concatenate([tin[0, 0], tin[1, 0], tin[0, 1], tin[1, 1]], axis=0)
             re, im = cmul(left, xmate[0], xmate[1])
-            trow[0, 0] = re
-            trow[0, 1] = im
+            for h in range(2):
+                trow[0, h, 0] = re[h * few:(h + 1) * few]
+                trow[0, h, 1] = im[h * few:(h + 1) * few]
 
         encode(0)
         for i in range(ga):
@@ -536,7 +629,9 @@
             copy.wait_recv()
 
     for i in range(ga):
-        tfull[:, i * rows:(i + 1) * rows, :] = decoded(tcodes[i], tscales[i]).reshape(2, rows, nb)
+        lines = decoded(tcodes[i], tscales[i]).reshape(2, 2, few, nb)
+        for h in range(2):
+            tfull[:, i * rows + h * few:i * rows + (h + 1) * few, :] = lines[h]
 
     phase("w")
     out_copy = pltpu.make_async_copy(tfull, transport, out_sem)
@@ -568,17 +663,13 @@
 
     phase("drain")
     for b in range(blocks):
-        for r in range(2):
-            nb_copy(b, r).wait_send()
-
-        @pl.when(odd == 1)
-        def _():
-            for r in range(2, 4):
-                nb_copy(b, r).wait_send()
-
+        nb_each(lambda copy: copy.wait_send(), b, True)
         for i in range(ga - 1):
             m_copy(b, i).wait_send()
-            e_copy(b, i).wait_send()
+    for span in range(2):
+        for i in range(ga - 1):
+            for copy in e_copies(span, i):
+                copy.wait_send()
     for i in range(ga - 2):
         for copy in piece_copies(i):
             copy.wait_send()
@@ -597,7 +688,8 @@
 
     @pl.when(k == 0)
     def _():
-        first.wait_send()
+        first(0).wait_send()
+        first(1).wait_send()
 
     @pl.when(jnp.logical_and(odd == 0, k > 0))
     def _():
@@ -605,8 +697,7 @@
 
     @pl.when(odd == 1)
     def _():
-        for r in range(2):
-            c_copy(r).wait_send()
+        c_each(lambda copy: copy.wait_send(), turn_on)
         for i in range(1, ga):
             for copy in same_copy(i):
                 copy.wait_send()
@@ -616,7 +707,8 @@
 
         @pl.when(k < ka - 1)
         def _():
-            onward.wait_send()
+            onward(0).wait_send()
+            onward(1).wait_send()
 
     out_copy.wait()
     phase(None)
@@ -642,7 +734,7 @@
             pltpu.VMEM((2 * half, nb), BF16),
             pltpu.VMEM((2 * nb, 2 * half), BF16),
             pltpu.VMEM((blocks, BANDS, 2 * half), BF16),
-            pltpu.VMEM((2, SHARED, nb), BF16),
+            pltpu.VMEM((2, TURNED, nb), BF16),
             pltpu.VMEM((2, blocks, BANDS, nb), F32),
             pltpu.VMEM((ga - 1, 2, blocks, brows, nb), F32),
             pltpu.VMEM((2, blocks, brows, nb), F32),
@@ -650,35 +742,39 @@
             pltpu.VMEM((3, 2, half, 2 * cols), BF16),
             pltpu.VMEM((ga, 2 * nb, 2 * cols), F32),
             pltpu.VMEM((ga - 2, 2 * nb, 2 * cols), I16),
-            pltpu.VMEM((ga - 2, 8, 2 * cols), F32),
+            pltpu.VMEM((ga - 2, 1, 2 * cols), F32),
             pltpu.VMEM((ga - 2, 2 * nb, 2 * cols), I16),
-            pltpu.VMEM((ga - 2, 8, 2 * cols), F32),
+            pltpu.VMEM((ga - 2, 1, 2 * cols), F32),
             pltpu.VMEM((2 * nb, 2 * cols), I16),
-            pltpu.VMEM((8, 2 * cols), F32),
+            pltpu.VMEM((1, 2 * cols), F32),
             pltpu.VMEM((2 * nb, 2 * cols), I16),
-            pltpu.VMEM((8, 2 * cols), F32),
+            pltpu.VMEM((1, 2 * cols), F32),
             pltpu.VMEM((blocks, 2, BANDS, nb), F32),
             pltpu.VMEM((blocks, ga - 1, 2, brows, nb), F32),
             pltpu.VMEM((blocks, 2, brows, nb), F32),
+            pltpu.VMEM((2 * blocks * brows, nb), I16),
+            pltpu.VMEM((2, 1, nb), F32),
+            pltpu.VMEM((ga, 2 * blocks * brows, nb), I16),
+            pltpu.VMEM((2, ga, 1, nb), F32),
             pltpu.VMEM((2, nb, nb), F32),
             pltpu.VMEM((2, nb, nb), F32),
             pltpu.VMEM((2, nb, nb), F32),
             pltpu.VMEM((nb, 2 * nb), BF16),
             pltpu.VMEM((nb, 2 * nb), BF16),
-            pltpu.VMEM((2, rows, nb), F32),
-            pltpu.VMEM((2, 2, rows, nb), F32),
+            pltpu.VMEM((2, 2, rows // 2, nb), F32),
+            pltpu.VMEM((2, 2, 2, rows // 2, nb), F32),
             pltpu.VMEM((2, 2 * rows, nb), I16),
-            pltpu.VMEM((2, 8, nb), F32),
+            pltpu.VMEM((2, 1, nb), F32),
             pltpu.VMEM((ga, 2 * rows, nb), I16),
-            pltpu.VMEM((ga, 8, nb), F32),
+            pltpu.VMEM((ga, 1, nb), F32),
             pltpu.VMEM((2, nb, nb), F32),
             pltpu.VMEM((ka, 1, 128), F32),
             pltpu.VMEM((ga, 1, 128), F32),
-            dma, dma((3, 2)), dma((blocks, 4)), dma((blocks, 4)), dma((2,)), dma((2,)),
-            dma((2,)), dma((2,)), dma((ga - 1,)), dma((ga - 1,)), dma, dma,
+            dma, dma((3, 2)), dma((blocks, 6)), dma((blocks, 6)), dma((2,)), dma((2,)),
+            dma((4,)), dma((4,)), dma((ga - 1,)), dma((ga - 1,)), dma, dma,
             dma((ga - 2, 2)), dma((ga - 2, 2)),
-            dma((blocks, ga - 1)), dma((blocks, ga - 1)), dma((blocks, ga - 1)), dma((blocks, ga - 1)),
-            dma, dma, dma, dma, dma((ga, 2)), dma((ga, 2)), dma((ga, 2)),
+            dma((blocks, ga - 1)), dma((blocks, ga - 1)), dma((2, ga - 1, 2)), dma((2, ga - 1, 2)),
+            dma, dma, dma((2,)), dma((2,)), dma((ga, 2)), dma((ga, 2)), dma((ga, 2)),
             dma((ka - 1,)), dma((ka - 1,)), dma((ga - 1,)), dma((ga - 1,)), dma,
             pltpu.SemaphoreType.REGULAR,
         ],

time: 88.3 us -> 84.8 us (0.960)
  Pallas kernels: 84.5 us -> 80.9 us
    pallas_call x1, Pallas kernels: 84.5 us -> 80.9 us  [local(): pl.pallas_call(functools.partial(kernel, ka, ga), out_shape=(jax.ShapeDty...]
where the time goes in v5:
time: 84.8 us; the launch traced here: 84.6 us
  Pallas kernels  80.9 us (95%)
  local copies, waits for them, and re-layouts  2.97 us (4%)
    pallas_call x1, Pallas kernels, local(): pl.pallas_call(functools.partial(kernel, ka, ga), out_shape=(jax.ShapeDty...  80.9 us
    unnamed x2, local copies, waits for them, and re-layouts  2.97 us

profile of v5, /device:TPU:0, one launch (start us, length us, event | category | flops | bytes accessed | tf_op | source)
XLA Modules:
  0.0 84.6 jit_solution(15610595455477270678)
XLA Ops:
  0.6 80.9 %string.1 = (f32[2,256,256]{2,1,0:T(8,128)}, f32[1,128]{1,0:T(1,128)}) custom-call(bf16[3840,256]{1,0:T(8,128)(2,1)} %bitcast.5, bf16[2,1920,1024]{2,1,0:T(8,128)(2,1)} %proj.1, bf16[2,1920,1024]{2,1,0:T(8,128)(2,1)} %deriv.1, s32[15,128]{1,0:T(8,128)} %bitcast.7, s32[8,128]{1,0:T(8,128)} %bitcast.8), custom_call_target="tpu_custom_call" | custom-call | tf_op jit(solution)/shard_map/string/pallas_call | solution.py:727
  81.6 1.9 %copy.9 = f32[1,2,256,256]{3,2,1,0:T(8,128)} copy(f32[1,2,256,256]{3,2,1,0:T(8,128)} %bitcast.6) | data formatting | bytes 1048576
  83.5 1.1 %copy.10 = f32[128]{0:T(128)} copy(f32[128]{0:T(128)} %bitcast.9) | data formatting | bytes 1024

commit v6 on v5

--- a/solution.py
+++ b/solution.py
@@ -87,6 +87,9 @@
             src_ref=source, dst_ref=target, send_sem=send, recv_sem=recv,
             device_id={"ka": to_k, "ga": to_g}, device_id_type=MESH)
 
+    def all_of(ref, sem):
+        pltpu.make_async_copy(ref, ref, sem).wait()
+
     own_load = pltpu.make_async_copy(coeffs, own, load_sem)
     own_load.start()
 
@@ -145,27 +148,35 @@
 
     def nb_copy(b, r):
         at = pl.ds(*ranges[r])
-        return remote(lhs.at[pl.ds(b * BANDS, BANDS), at], nbt.at[b, :, at], nb_send.at[b, r], nb_recv.at[b, r],
+        return remote(lhs.at[pl.ds(b * BANDS, BANDS), at], nbt.at[b, :, at], nb_send, nb_recv.at[b],
                       ka_at(ka - 1), g)
 
-    def nb_each(act, b, sent):
-        short = turn_back if sent else turn_on
-        whole = odd == 1 if sent else odd == 0
+    def by_class(turned, act):
+        @pl.when(turned)
+        def _():
+            act(least)
+
+        @pl.when(jnp.logical_and(odd == (0 if turned is turn_back else 1), jnp.logical_not(turned)))
+        def _():
+            act(kept)
+
+        @pl.when(odd == (1 if turned is turn_back else 0))
+        def _():
+            act(half)
+
+    for b in range(blocks):
         for r in (0, 1):
-            act(nb_copy(b, r))
-
-        @pl.when(jnp.logical_not(short))
+            nb_copy(b, r).start()
+
+        @pl.when(jnp.logical_not(turn_back))
         def _():
             for r in (2, 3):
-                act(nb_copy(b, r))
-
-        @pl.when(whole)
+                nb_copy(b, r).start()
+
+        @pl.when(odd == 1)
         def _():
             for r in (4, 5):
-                act(nb_copy(b, r))
-
-    for b in range(blocks):
-        nb_each(lambda copy: copy.start(), b, True)
+                nb_copy(b, r).start()
 
     phase("permute")
 
@@ -188,20 +199,26 @@
         first, count = ranges[2 + r]
         part_at = half * (r % 2)
         return remote(own.at[pl.ds(first, count)], cnat.at[r % 2, pl.ds(first - part_at - least, count)],
-                      c_send.at[r], c_recv.at[r], ka_at(1), g)
-
-    def c_each(act, short):
+                      c_send, c_recv, ka_at(1), g)
+
+    @pl.when(odd == 1)
+    def _():
         for r in (2, 3):
-            act(c_copy(r))
-
+            c_copy(r).start()
+
+        @pl.when(turn_on)
+        def _():
+            for r in (0, 1):
+                c_copy(r).start()
+
+    def c_all(sem, short):
         @pl.when(short)
         def _():
-            for r in (0, 1):
-                act(c_copy(r))
-
-    @pl.when(odd == 1)
-    def _():
-        c_each(lambda copy: copy.start(), turn_on)
+            all_of(cnat, sem)
+
+        @pl.when(jnp.logical_not(short))
+        def _():
+            all_of(cnat.at[:, pl.ds(kept - least, SHARED)], sem)
 
     def piece_to(i):
         across = (i // 4) * (1 - lax.rem(i, 2))
@@ -209,8 +226,8 @@
 
     def piece_copies(i):
         return (
-            remote(pieces.at[i], in_pieces.at[i], p_send.at[i, 0], p_recv.at[i, 0], k, piece_to(i)),
-            remote(scales.at[i], in_scales.at[i], p_send.at[i, 1], p_recv.at[i, 1], k, piece_to(i)),
+            remote(pieces.at[i], in_pieces.at[i], p_send.at[0], p_recv.at[lax.max(i, 3) - 3, 0], k, piece_to(i)),
+            remote(scales.at[i], in_scales.at[i], p_send.at[1], p_recv.at[lax.max(i, 3) - 3, 1], k, piece_to(i)),
         )
 
     def coded(values):
@@ -262,7 +279,7 @@
     def m_copy(b, i):
         target = ga_at(1 + i)
         at = pl.ds(pl.multiple_of(target * brows, brows), brows)
-        return remote(mpart.at[b, :, at, :], mrows.at[b, i], m_send.at[b, i], m_recv.at[b, i], k, target)
+        return remote(mpart.at[b, :, at, :], mrows.at[b, i], m_send.at[b], m_recv.at[b], k, target)
 
     def intersect(b):
         phase(f"nb_wait{b}")
@@ -273,32 +290,23 @@
             by_im = dot(jnp.concatenate([im, -re], axis=0), own[half:half + count, :])
             mpart[b] = (by_re + by_im).reshape(2, BANDS, nb)
 
-        nb_each(lambda copy: copy.wait_recv(), b, False)
-
-        @pl.when(turn_on)
-        def _():
-            over(least)
-
-        @pl.when(jnp.logical_and(odd == 1, jnp.logical_not(turn_on)))
-        def _():
-            over(kept)
-
-        @pl.when(odd == 0)
-        def _():
-            over(half)
-
+        def here(count):
+            all_of(nbt.at[b, :, pl.ds(0, 2 * count)], nb_recv.at[b])
+            over(count)
+
+        by_class(turn_on, here)
         phase(f"m_dot{b}")
         for i in range(ga - 1):
             m_copy(b, i).start()
 
     def a_copy(i):
         at = pl.ds(pl.multiple_of(ga_at(1 + i) * brows, brows), brows)
-        return remote(taken.at[:, :, at, :], taken_rows.at[i], a_send.at[i], a_recv.at[i], k, ga_at(1 + i))
+        return remote(taken.at[:, :, at, :], taken_rows.at[i], a_send, a_recv, k, ga_at(1 + i))
 
     s_copy = remote(taken_sum, taken_in, s_send, s_recv, ka_at(ka - 1), g)
 
     def take():
-        c_each(lambda copy: copy.wait_recv(), turn_back)
+        c_all(c_recv, turn_back)
 
         def from_wave(first):
             out = dot(lhs[:, first:half], cnat[0, first - least:])
@@ -318,8 +326,8 @@
 
     def give_back():
         out = taken[:, :, pl.ds(pl.multiple_of(g * brows, brows), brows), :]
+        all_of(taken_rows, a_recv)
         for i in range(ga - 1):
-            a_copy(i).wait_recv()
             out = out + taken_rows[i]
         taken_sum[...] = out
         s_copy.start()
@@ -334,8 +342,8 @@
     def e_copies(span, i):
         to = ga_at(1 + i)
         return (
-            remote(ecode.at[span_rows(span)], ecodes.at[g, span_rows(span)], e_send.at[span, i, 0], e_recv.at[span, i, 0], k, to),
-            remote(escale.at[span], escales.at[span, g], e_send.at[span, i, 1], e_recv.at[span, i, 1], k, to),
+            remote(ecode.at[span_rows(span)], ecodes.at[g, span_rows(span)], e_send.at[span, 0], e_recv.at[span, 0], k, to),
+            remote(escale.at[span], escales.at[span, g], e_send.at[span, 1], e_recv.at[span, 1], k, to),
         )
 
     def spread(span):
@@ -352,8 +360,8 @@
     def settle(b):
         phase(f"m_rs{b}")
         total = mpart[b, :, pl.ds(pl.multiple_of(g * brows, brows), brows), :]
+        all_of(mrows.at[b], m_recv.at[b])
         for i in range(ga - 1):
-            m_copy(b, i).wait_recv()
             total = total + mrows[b, i]
         erow[b] = total
 
@@ -425,10 +433,12 @@
         take()
 
     phase("e_ag")
-    for span in range(2):
-        for i in range(ga - 1):
-            for copy in e_copies(span, i):
-                copy.wait_recv()
+    def e_all(sem):
+        for span in range(2):
+            all_of(ecodes.at[pl.ds(0, ga - 1), span_rows(span)], sem.at[span, 0])
+            all_of(escales.at[span, pl.ds(0, ga - 1)], sem.at[span, 1])
+
+    e_all(e_recv)
     for i in range(ga):
         for b in range(blocks):
             span = b // (blocks - 1)
@@ -464,14 +474,14 @@
 
     def same_copy(i):
         return (
-            remote(tcode.at[1], tcodes.at[g], g_send.at[i, 0], g_recv.at[i, 0], k, ga_at(i)),
-            remote(tscale.at[1], tscales.at[g], g_send.at[i, 1], g_recv.at[i, 1], k, ga_at(i)),
+            remote(tcode.at[1], tcodes.at[g], g_send.at[0], g_recv.at[0], k, ga_at(i)),
+            remote(tscale.at[1], tscales.at[g], g_send.at[1], g_recv.at[1], k, ga_at(i)),
         )
 
     def mate_copy(i):
         return (
-            remote(tcode.at[0], tcodes.at[g], h_send.at[i, 0], g_recv.at[i, 0], mate, ga_at(i)),
-            remote(tscale.at[0], tscales.at[g], h_send.at[i, 1], g_recv.at[i, 1], mate, ga_at(i)),
+            remote(tcode.at[0], tcodes.at[g], h_send.at[0], g_recv.at[0], mate, ga_at(i)),
+            remote(tscale.at[0], tscales.at[g], h_send.at[1], g_recv.at[1], mate, ga_at(i)),
         )
 
     def encode(which):
@@ -516,9 +526,10 @@
             send(5, 6)
 
         phase("p_wait")
-        for i in (0, 1, 2, 3, 5):
-            for copy in piece_copies(i):
-                copy.wait_recv()
+        all_of(in_pieces.at[pl.ds(0, 4)], p_recv.at[0, 0])
+        all_of(in_scales.at[pl.ds(0, 4)], p_recv.at[0, 1])
+        for copy in piece_copies(5):
+            copy.wait_recv()
         phase("p_sum")
         out = part[ga - 2]
         for i in (0, 1):
@@ -619,14 +630,17 @@
     atom_column = jnp.broadcast_to(atoms[pl.ds(g, 1), :].astype(F32), (cols, 128)).T
 
     phase("t_ag")
-    for i in range(1, ga):
-        for copy in same_copy(i):
-            copy.wait_recv()
+    def t_all(sem, count):
+        all_of(tcodes.at[pl.ds(0, count)], sem.at[0])
+        all_of(tscales.at[pl.ds(0, count)], sem.at[1])
+
+    @pl.when(odd == 1)
+    def _():
+        t_all(g_recv, ga - 1)
 
     @pl.when(odd == 0)
     def _():
-        for copy in mate_copy(0):
-            copy.wait_recv()
+        t_all(g_recv, ga)
 
     for i in range(ga):
         lines = decoded(tcodes[i], tscales[i]).reshape(2, 2, few, nb)
@@ -643,47 +657,37 @@
     fka[k] = force
 
     def along_ka(i):
-        return remote(fka.at[k], fka.at[k], f_send.at[i], f_recv.at[i], ka_at(1 + i), g)
+        return remote(fka.at[k], fka.at[k], f_send, f_recv, ka_at(1 + i), g)
 
     def along_ga(i):
-        return remote(fga.at[g], fga.at[g], l_send.at[i], l_recv.at[i], k, ga_at(1 + i))
+        return remote(fga.at[g], fga.at[g], l_send, l_recv, k, ga_at(1 + i))
 
     phase("f_ka")
     for i in range(ka - 1):
         along_ka(i).start()
-    for i in range(ka - 1):
-        along_ka(i).wait_recv()
+    all_of(fka.at[pl.ds(0, ka - 1)], f_recv)
     phase("f_ga")
     fga[g] = jnp.sum(fka[...], axis=0)
     for i in range(ga - 1):
         along_ga(i).start()
-    for i in range(ga - 1):
-        along_ga(i).wait_recv()
+    all_of(fga.at[pl.ds(0, ga - 1)], l_recv)
     forces[...] = jnp.sum(fga[...], axis=0)
 
     phase("drain")
+    by_class(turn_back, lambda count: all_of(nbt.at[:, :, pl.ds(0, 2 * count)], nb_send))
     for b in range(blocks):
-        nb_each(lambda copy: copy.wait_send(), b, True)
-        for i in range(ga - 1):
-            m_copy(b, i).wait_send()
-    for span in range(2):
-        for i in range(ga - 1):
-            for copy in e_copies(span, i):
-                copy.wait_send()
-    for i in range(ga - 2):
-        for copy in piece_copies(i):
-            copy.wait_send()
+        all_of(mrows.at[b], m_send.at[b])
+    e_all(e_send)
+    all_of(in_pieces, p_send.at[0])
+    all_of(in_scales, p_send.at[1])
     for copy in z_copies:
         copy.wait_send()
-    for i in range(ga - 1):
-        along_ga(i).wait_send()
-    for i in range(ka - 1):
-        along_ka(i).wait_send()
+    all_of(fga.at[pl.ds(0, ga - 1)], l_send)
+    all_of(fka.at[pl.ds(0, ka - 1)], f_send)
 
     @pl.when(odd == 0)
     def _():
-        for i in range(ga - 1):
-            a_copy(i).wait_send()
+        all_of(taken_rows, a_send)
         s_copy.wait_send()
 
     @pl.when(k == 0)
@@ -697,13 +701,9 @@
 
     @pl.when(odd == 1)
     def _():
-        c_each(lambda copy: copy.wait_send(), turn_on)
-        for i in range(1, ga):
-            for copy in same_copy(i):
-                copy.wait_send()
-        for i in range(ga):
-            for copy in mate_copy(i):
-                copy.wait_send()
+        c_all(c_send, turn_on)
+        t_all(g_send, ga - 1)
+        t_all(h_send, ga)
 
         @pl.when(k < ka - 1)
         def _():
@@ -770,12 +770,9 @@
             pltpu.VMEM((2, nb, nb), F32),
             pltpu.VMEM((ka, 1, 128), F32),
             pltpu.VMEM((ga, 1, 128), F32),
-            dma, dma((3, 2)), dma((blocks, 6)), dma((blocks, 6)), dma((2,)), dma((2,)),
-            dma((4,)), dma((4,)), dma((ga - 1,)), dma((ga - 1,)), dma, dma,
-            dma((ga - 2, 2)), dma((ga - 2, 2)),
-            dma((blocks, ga - 1)), dma((blocks, ga - 1)), dma((2, ga - 1, 2)), dma((2, ga - 1, 2)),
-            dma, dma, dma((2,)), dma((2,)), dma((ga, 2)), dma((ga, 2)), dma((ga, 2)),
-            dma((ka - 1,)), dma((ka - 1,)), dma((ga - 1,)), dma((ga - 1,)), dma,
+            dma, dma((3, 2)), dma, dma((blocks,)), dma((2,)), dma((2,)), dma, dma, dma, dma, dma, dma,
+            dma((2,)), dma((3, 2)), dma((blocks,)), dma((blocks,)), dma((2, 2)), dma((2, 2)),
+            dma, dma, dma((2,)), dma((2,)), dma((2,)), dma((2,)), dma((2,)), dma, dma, dma, dma, dma,
             pltpu.SemaphoreType.REGULAR,
         ],
         compiler_params=pltpu.CompilerParams(

time: 84.8 us -> 82.2 us (0.969)
  Pallas kernels: 80.9 us -> 78.4 us
    pallas_call x1, Pallas kernels: 80.9 us -> 78.4 us  [local(): pl.pallas_call(functools.partial(kernel, ka, ga), out_shape=(jax.ShapeDty...]
where the time goes in v6:
time: 82.2 us; the launch traced here: 82 us
  Pallas kernels  78.4 us (95%)
  local copies, waits for them, and re-layouts  2.97 us (4%)
    pallas_call x1, Pallas kernels, local(): pl.pallas_call(functools.partial(kernel, ka, ga), out_shape=(jax.ShapeDty...  78.4 us
    unnamed x2, local copies, waits for them, and re-layouts  2.97 us

profile of v6, /device:TPU:0, one launch (start us, length us, event | category | flops | bytes accessed | tf_op | source)
XLA Modules:
  0.0 82.0 jit_solution(1967950059217253173)
XLA Ops:
  0.6 78.4 %string.1 = (f32[2,256,256]{2,1,0:T(8,128)}, f32[1,128]{1,0:T(1,128)}) custom-call(bf16[3840,256]{1,0:T(8,128)(2,1)} %bitcast.5, bf16[2,1920,1024]{2,1,0:T(8,128)(2,1)} %proj.1, bf16[2,1920,1024]{2,1,0:T(8,128)(2,1)} %deriv.1, s32[15,128]{1,0:T(8,128)} %bitcast.7, s32[8,128]{1,0:T(8,128)} %bitcast.8), custom_call_target="tpu_custom_call" | custom-call | tf_op jit(solution)/shard_map/string/pallas_call | solution.py:727
  79.1 1.9 %copy.9 = f32[1,2,256,256]{3,2,1,0:T(8,128)} copy(f32[1,2,256,256]{3,2,1,0:T(8,128)} %bitcast.6) | data formatting | bytes 1048576
  80.9 1.1 %copy.10 = f32[128]{0:T(128)} copy(f32[128]{0:T(128)} %bitcast.9) | data formatting | bytes 1024

commit v7 on v6

--- a/solution.py
+++ b/solution.py
@@ -45,11 +45,11 @@
 
 
 def kernel(
-    ka, ga, coeffs, proj, deriv, shift, atoms, transport, forces,
+    ka, ga, coeffs, proj, deriv, shift, atoms, tfull, forces,
     own, moved, lhs, nbt, cnat, taken, taken_rows, taken_sum, taken_in, rhs, part, pieces, scales, in_pieces, in_scales, z_piece, z_scale, z_in, z_in_scale, mpart, mrows, erow, ecode, escale, ecodes, escales, efull,
-    xfull, xmate, qhigh, qlow, tin, trow, tcode, tscale, tcodes, tscales, tfull, fka, fga,
+    xfull, xmate, qhigh, qlow, tin, trow, tcode, tscale, tcodes, tscales, fka, fga,
     load_sem, rhs_sem, nb_send, nb_recv, z_send, z_recv, c_send, c_recv, a_send, a_recv, s_send, s_recv, p_send, p_recv, m_send, m_recv, e_send, e_recv,
-    x_send, x_recv, t_send, t_recv, g_send, g_recv, h_send, f_send, f_recv, l_send, l_recv, out_sem, ready_sem,
+    x_send, x_recv, t_send, t_recv, g_send, g_recv, h_send, f_send, f_recv, l_send, l_recv, ready_sem,
 ):
     phases = []
 
@@ -648,8 +648,6 @@
             tfull[:, i * rows + h * few:i * rows + (h + 1) * few, :] = lines[h]
 
     phase("w")
-    out_copy = pltpu.make_async_copy(tfull, transport, out_sem)
-    out_copy.start()
     w_re, w_im = cmul(b_both, tfull[0], tfull[1])
     per_proj = jnp.sum(d_re * w_im - d_im * w_re, axis=1, keepdims=True) * (1.0 / ka)
     atom_ids = lax.broadcasted_iota(jnp.int32, (cols, 128), 1).astype(F32)
@@ -710,7 +708,6 @@
             onward(0).wait_send()
             onward(1).wait_send()
 
-    out_copy.wait()
     phase(None)
 
 
@@ -728,7 +725,7 @@
         functools.partial(kernel, ka, ga),
         out_shape=(jax.ShapeDtypeStruct((2, nb, nb), F32), jax.ShapeDtypeStruct((1, 128), F32)),
         in_specs=[anywhere, anywhere, anywhere, vmem, vmem],
-        out_specs=(anywhere, vmem),
+        out_specs=(vmem, vmem),
         scratch_shapes=[
             pltpu.VMEM((2 * half, nb), BF16),
             pltpu.VMEM((2 * half, nb), BF16),
@@ -767,16 +764,15 @@
             pltpu.VMEM((2, 1, nb), F32),
             pltpu.VMEM((ga, 2 * rows, nb), I16),
             pltpu.VMEM((ga, 1, nb), F32),
-            pltpu.VMEM((2, nb, nb), F32),
             pltpu.VMEM((ka, 1, 128), F32),
             pltpu.VMEM((ga, 1, 128), F32),
             dma, dma((3, 2)), dma, dma((blocks,)), dma((2,)), dma((2,)), dma, dma, dma, dma, dma, dma,
             dma((2,)), dma((3, 2)), dma((blocks,)), dma((blocks,)), dma((2, 2)), dma((2, 2)),
-            dma, dma, dma((2,)), dma((2,)), dma((2,)), dma((2,)), dma((2,)), dma, dma, dma, dma, dma,
+            dma, dma, dma((2,)), dma((2,)), dma((2,)), dma((2,)), dma((2,)), dma, dma, dma, dma,
             pltpu.SemaphoreType.REGULAR,
         ],
         compiler_params=pltpu.CompilerParams(
-            collective_id=0, has_side_effects=True, vmem_limit_bytes=60 * 1024 * 1024),
+            collective_id=0, has_side_effects=True, vmem_limit_bytes=53 * 1024 * 1024),
         name="string",
     )(
         coeffs.reshape(2 * half, nb), projectors, proj_deriv,

time: 82.2 us -> 80.7 us (0.982)
  Pallas kernels: 78.4 us -> 77.1 us
    pallas_call x1, Pallas kernels: 78.4 us -> 77.1 us  [local(): pl.pallas_call(functools.partial(kernel, ka, ga), out_shape=(jax.ShapeDty...]
    unnamed x2 -> x6, local copies, waits for them, and re-layouts: 2.97 us -> 2.68 us
where the time goes in v7:
time: 80.7 us; the launch traced here: 80.5 us
  Pallas kernels  77.1 us (96%)
  local copies, waits for them, and re-layouts  2.68 us (3%)
    pallas_call x1, Pallas kernels, local(): pl.pallas_call(functools.partial(kernel, ka, ga), out_shape=(jax.ShapeDty...  77.1 us
    unnamed x6, local copies, waits for them, and re-layouts  2.68 us

profile of v7, /device:TPU:0, one launch (start us, length us, event | category | flops | bytes accessed | tf_op | source)
XLA Modules:
  0.0 80.5 jit_solution(2298705530352028159)
XLA Ops:
  0.6 0.0 copy-start
  0.6 0.7 copy-done
  1.3 0.0 copy-start.1
  1.3 0.7 copy-done.1
  2.0 77.1 %string.1 = (f32[2,256,256]{2,1,0:T(8,128)S(1)}, f32[1,128]{1,0:T(1,128)S(1)}) custom-call(bf16[3840,256]{1,0:T(8,128)(2,1)} %bitcast.9, bf16[2,1920,1024]{2,1,0:T(8,128)(2,1)} %proj.1, bf16[2,1920,1024]{2,1,0:T(8,128)(2,1)} %deriv.1, s32[15,128]{1,0:T(8,128)S(1)} %bitcast.6, s32[8,128]{1,0:T(8,128)S(1)} %bitcast.7), custom_call_target="tpu_custom_call" | custom-call | tf_op jit(solution)/shard_map/string/pallas_call | solution.py:724
  79.2 0.8 copy.9
  80.0 0.5 copy.10
Async XLA Ops:
  0.6 0.7 copy-start
  1.3 0.7 copy-start.1

commit v8 on v7

--- a/solution.py
+++ b/solution.py
@@ -12,8 +12,8 @@
 BF16 = jnp.bfloat16
 I16 = jnp.int16
 BANDS = 64
-SHARED = 640
-TURNED = 1024
+SHARED = 768
+TURNED = 896
 EARLY = 2
 FIRST = 4
 HURRY = 12

time: 80.7 us -> 79.4 us (0.984)
  Pallas kernels: 77.1 us -> 75.9 us
    pallas_call x1, Pallas kernels: 77.1 us -> 75.9 us  [local(): pl.pallas_call(functools.partial(kernel, ka, ga), out_shape=(jax.ShapeDty...]
where the time goes in v8:
time: 79.4 us; the launch traced here: 79.2 us
  Pallas kernels  75.9 us (96%)
  local copies, waits for them, and re-layouts  2.68 us (3%)
    pallas_call x1, Pallas kernels, local(): pl.pallas_call(functools.partial(kernel, ka, ga), out_shape=(jax.ShapeDty...  75.9 us
    unnamed x6, local copies, waits for them, and re-layouts  2.68 us

profile of v8, /device:TPU:0, one launch (start us, length us, event | category | flops | bytes accessed | tf_op | source)
XLA Modules:
  0.0 79.2 jit_solution(3798835069031861355)
XLA Ops:
  0.6 0.0 copy-start
  0.6 0.7 copy-done
  1.3 0.0 copy-start.1
  1.3 0.7 copy-done.1
  2.0 75.9 %string.1 = (f32[2,256,256]{2,1,0:T(8,128)S(1)}, f32[1,128]{1,0:T(1,128)S(1)}) custom-call(bf16[3840,256]{1,0:T(8,128)(2,1)} %bitcast.9, bf16[2,1920,1024]{2,1,0:T(8,128)(2,1)} %proj.1, bf16[2,1920,1024]{2,1,0:T(8,128)(2,1)} %deriv.1, s32[15,128]{1,0:T(8,128)S(1)} %bitcast.6, s32[8,128]{1,0:T(8,128)S(1)} %bitcast.7), custom_call_target="tpu_custom_call" | custom-call | tf_op jit(solution)/shard_map/string/pallas_call | solution.py:724
  77.9 0.8 %copy.9 = f32[1,2,256,256]{3,2,1,0:T(8,128)} copy(f32[1,2,256,256]{3,2,1,0:T(8,128)S(1)} %bitcast.5) | data formatting | bytes 1048576
  78.7 0.5 copy.10
Async XLA Ops:
  0.6 0.7 copy-start
  1.3 0.7 copy-start.1

commit v9 on v8

--- a/solution.py
+++ b/solution.py
@@ -16,6 +16,7 @@
 TURNED = 896
 EARLY = 2
 FIRST = 4
+FAR_FIRST = (3, 5, 4, 7, 1, 2, 6)
 HURRY = 12
 LATE = 10
 
@@ -296,8 +297,8 @@
 
         by_class(turn_on, here)
         phase(f"m_dot{b}")
-        for i in range(ga - 1):
-            m_copy(b, i).start()
+        for step in FAR_FIRST:
+            m_copy(b, step - 1).start()
 
     def a_copy(i):
         at = pl.ds(pl.multiple_of(ga_at(1 + i) * brows, brows), brows)
@@ -321,8 +322,8 @@
         def _():
             from_wave(kept)
 
-        for i in range(ga - 1):
-            a_copy(i).start()
+        for step in FAR_FIRST:
+            a_copy(step - 1).start()
 
     def give_back():
         out = taken[:, :, pl.ds(pl.multiple_of(g * brows, brows), brows), :]
@@ -351,8 +352,8 @@
         code, scale = coded(erow[first:last].reshape(2 * brows * (last - first), nb))
         ecode[span_rows(span), :] = code
         escale[span] = scale
-        for i in range(ga - 1):
-            for copy in e_copies(span, i):
+        for step in FAR_FIRST:
+            for copy in e_copies(span, step - 1):
                 copy.start()
         ecodes[g, span_rows(span), :] = code
         escales[span, g] = scale
@@ -590,7 +591,7 @@
                 onward(h).start()
 
         encode(1)
-        for i in range(1, ga):
+        for i in FAR_FIRST:
             for copy in same_copy(i):
                 copy.start()
         tcodes[g] = tcode[1]
@@ -611,7 +612,7 @@
                 trow[0, h, 1] = im[h * few:(h + 1) * few]
 
         encode(0)
-        for i in range(ga):
+        for i in FAR_FIRST + (0,):
             for copy in mate_copy(i):
                 copy.start()
 
@@ -666,8 +667,8 @@
     all_of(fka.at[pl.ds(0, ka - 1)], f_recv)
     phase("f_ga")
     fga[g] = jnp.sum(fka[...], axis=0)
-    for i in range(ga - 1):
-        along_ga(i).start()
+    for step in FAR_FIRST:
+        along_ga(step - 1).start()
     all_of(fga.at[pl.ds(0, ga - 1)], l_recv)
     forces[...] = jnp.sum(fga[...], axis=0)
 

time: 79.4 us -> 78.5 us (0.989)
  Pallas kernels: 75.9 us -> 74.9 us
    pallas_call x1, Pallas kernels: 75.9 us -> 74.9 us  [local(): pl.pallas_call(functools.partial(kernel, ka, ga), out_shape=(jax.ShapeDty...]
where the time goes in v9:
time: 78.5 us; the launch traced here: 78.3 us
  Pallas kernels  74.9 us (95%)
  local copies, waits for them, and re-layouts  2.68 us (3%)
    pallas_call x1, Pallas kernels, local(): pl.pallas_call(functools.partial(kernel, ka, ga), out_shape=(jax.ShapeDty...  74.9 us
    unnamed x6, local copies, waits for them, and re-layouts  2.68 us

profile of v9, /device:TPU:0, one launch (start us, length us, event | category | flops | bytes accessed | tf_op | source)
XLA Modules:
  0.0 78.3 jit_solution(517173908753547296)
XLA Ops:
  0.6 0.0 copy-start
  0.6 0.7 copy-done
  1.3 0.0 copy-start.1
  1.3 0.7 copy-done.1
  2.0 74.9 %string.1 = (f32[2,256,256]{2,1,0:T(8,128)S(1)}, f32[1,128]{1,0:T(1,128)S(1)}) custom-call(bf16[3840,256]{1,0:T(8,128)(2,1)} %bitcast.9, bf16[2,1920,1024]{2,1,0:T(8,128)(2,1)} %proj.1, bf16[2,1920,1024]{2,1,0:T(8,128)(2,1)} %deriv.1, s32[15,128]{1,0:T(8,128)S(1)} %bitcast.6, s32[8,128]{1,0:T(8,128)S(1)} %bitcast.7), custom_call_target="tpu_custom_call" | custom-call | tf_op jit(solution)/shard_map/string/pallas_call | solution.py:725
  77.0 0.8 %copy.9 = f32[1,2,256,256]{3,2,1,0:T(8,128)} copy(f32[1,2,256,256]{3,2,1,0:T(8,128)S(1)} %bitcast.5) | data formatting | bytes 1048576
  77.8 0.5 copy.10
Async XLA Ops:
  0.6 0.7 copy-start
  1.3 0.7 copy-start.1

commit v10 on v9

--- a/solution.py
+++ b/solution.py
@@ -662,8 +662,8 @@
         return remote(fga.at[g], fga.at[g], l_send, l_recv, k, ga_at(1 + i))
 
     phase("f_ka")
-    for i in range(ka - 1):
-        along_ka(i).start()
+    for step in sorted(range(1, ka), key=lambda step: abs(step % (ka // 2) - ka // 4)):
+        along_ka(step - 1).start()
     all_of(fka.at[pl.ds(0, ka - 1)], f_recv)
     phase("f_ga")
     fga[g] = jnp.sum(fka[...], axis=0)

time: 78.5 us -> 78.5 us (level)
  no operation moved by 1% of the time
where the time goes in v10:
time: 78.5 us; the launch traced here: 78.3 us
  Pallas kernels  75 us (96%)
  local copies, waits for them, and re-layouts  2.68 us (3%)
    pallas_call x1, Pallas kernels, local(): pl.pallas_call(functools.partial(kernel, ka, ga), out_shape=(jax.ShapeDty...  75 us
    unnamed x6, local copies, waits for them, and re-layouts  2.68 us

profile of v10, /device:TPU:0, one launch (start us, length us, event | category | flops | bytes accessed | tf_op | source)
XLA Modules:
  0.0 78.3 jit_solution(13591724028641139080)
XLA Ops:
  0.6 0.0 copy-start
  0.6 0.7 copy-done
  1.3 0.0 copy-start.1
  1.3 0.7 copy-done.1
  2.0 75.0 %string.1 = (f32[2,256,256]{2,1,0:T(8,128)S(1)}, f32[1,128]{1,0:T(1,128)S(1)}) custom-call(bf16[3840,256]{1,0:T(8,128)(2,1)} %bitcast.9, bf16[2,1920,1024]{2,1,0:T(8,128)(2,1)} %proj.1, bf16[2,1920,1024]{2,1,0:T(8,128)(2,1)} %deriv.1, s32[15,128]{1,0:T(8,128)S(1)} %bitcast.6, s32[8,128]{1,0:T(8,128)S(1)} %bitcast.7), custom_call_target="tpu_custom_call" | custom-call | tf_op jit(solution)/shard_map/string/pallas_call | solution.py:725
  77.0 0.8 %copy.9 = f32[1,2,256,256]{3,2,1,0:T(8,128)} copy(f32[1,2,256,256]{3,2,1,0:T(8,128)S(1)} %bitcast.5) | data formatting | bytes 1048576
  77.8 0.5 copy.10
Async XLA Ops:
  0.6 0.7 copy-start
  1.3 0.7 copy-start.1
